TPU v7x, 256 devices: a whole 4x4x8 slice. The times are simulated.
256 devices in a mesh: feat: 64 (over y, x, z_lo), rep: 4 (over z_hi, core).
Axes of the slice: x: 4, y: 4, z: 8 (z_hi: 2, z_lo: 4; z = z_hi * 4 + z_lo), core: 2. Of those that a mesh axis runs over, the one named last changes fastest.
Arguments:
- features: bfloat16 [4, 64, 1024, 512], P('rep', None, 'feat'), may hold values from -6 to 6
- adjacency_one: int32 [4, 64, 5, 16, 512], P('rep'), may hold values from 0 to 65535, as said below
- pre_hidden: bfloat16 [4, 64, 256, 256], P('rep', 'feat'), may hold values from -6 to 6
- adjacency_two: int32 [4, 64, 5, 8, 256], P('rep', 'feat'), may hold values from 0 to 65535, as said below
- weight_two: bfloat16 [6, 256, 256], replicated, may hold values from -0.375 to 0.375
- out_grad: bfloat16 [4, 64, 128, 256], P('rep', 'feat'), may hold values from -6 to 6
Outputs:
- grad_w1: float32 [6, 1024, 256], P(None, 'feat')
- grad_b1: float32 [256], replicated
- grad_w2: float32 [6, 256, 256], replicated
- grad_b2: float32 [256], replicated
Inputs may be any that keep to these rules, and one draw needn't show every extreme that they name: `adjacency_one`: bit k, k below 16, of word (w, n) is the entry of destination row 16 w + k and source column n; higher bits are zero; some rows are empty. `adjacency_two`: bit k, k below 16, of word (w, n) is the entry of seed row 16 w + k and source column n; higher bits are zero; some rows are empty.
All inputs are finite; a program needn't handle non-finite values.
Results may differ from a plain program's by a relative error of at most 0.0041.
Values may be sent and summed in bfloat16 or wider, within the bound.
A program may use at most 128 MiB of HBM per device.

v0:
```python
import math

import jax
import jax.numpy as jnp
from jax import lax
from jax.sharding import Mesh
from jax.sharding import PartitionSpec as P

FEAT = ("feat_0", "feat_1", "feat_2")
FEAT_REP = ("feat_0", "feat_1", "feat_2", "rep")


def in_order(tiles, dim):
    tiles = jnp.moveaxis(tiles, 0, dim)
    lengths = tiles.shape
    return tiles.reshape(*lengths[:dim], lengths[dim] * lengths[dim + 1], *lengths[dim + 2 :])


def all_blocks(x, axes, order):
    tiles = x
    for k in order:
        tiles = lax.all_gather(tiles, axes[k])
    done = order[::-1]
    back = [done.index(k) for k in range(len(axes))]
    tiles = tiles.transpose(*back, *range(len(axes), tiles.ndim))
    return tiles.reshape(-1, *x.shape)


def gather_axes(x, axes, order, dim):
    return in_order(all_blocks(x, axes, order), dim)


def copy_for_each(x, axis):
    copies = jnp.broadcast_to(x, (lax.axis_size(axis), *x.shape))
    return lax.all_to_all(copies, axis, split_axis=0, concat_axis=0, tiled=True)


def of_everyone(x, axis):
    return copy_for_each(x, axis).sum(axis=0)


def unpack(packed):
    shifts = jnp.arange(16, dtype=jnp.int32)
    spread = jnp.bitwise_and(jnp.right_shift(packed[..., None, :], shifts[:, None]), 1)
    dense = spread.reshape(packed.shape[:-2] + (packed.shape[-2] * 16, packed.shape[-1]))
    degree = jnp.sum(dense, axis=-1).astype(jnp.float32)
    return (dense.astype(jnp.bfloat16), 1.0 / jnp.maximum(degree, 1.0))


def upper_layer(pre_rows, words_two, grad_rows, weight_two, factor):
    hidden = jnp.maximum(pre_rows, 0)
    seed_count = grad_rows.shape[0]
    matrix, inverse = unpack(words_two)
    mixed = (
        jnp.einsum("rsd,dh->rsh", matrix, hidden, preferred_element_type=jnp.float32)
        * inverse[..., None]
    ).astype(jnp.bfloat16)
    scaled = grad_rows.astype(jnp.float32) * factor
    scaled_low = scaled.astype(jnp.bfloat16)
    grad_rel = jnp.einsum("rsh,sk->rhk", mixed, scaled_low, preferred_element_type=jnp.float32)
    grad_self = jnp.einsum(
        "sh,sk->hk", hidden[:seed_count], scaled_low, preferred_element_type=jnp.float32
    )
    weight_grad = jnp.concatenate([grad_self[None], grad_rel], 0)
    backed = (
        jnp.einsum("sk,rhk->rsh", scaled_low, weight_two[1:], preferred_element_type=jnp.float32)
        * inverse[..., None]
    ).astype(jnp.bfloat16)
    spread_back = jnp.einsum("rsd,rsh->dh", matrix, backed, preferred_element_type=jnp.float32)
    own_part = jnp.einsum(
        "sk,hk->sh", scaled_low, weight_two[0], preferred_element_type=jnp.float32
    )
    hidden_total = spread_back + jnp.pad(own_part, ((0, hidden.shape[0] - seed_count), (0, 0)))
    hidden_grad = jnp.where(pre_rows > 0, hidden_total, 0.0).astype(jnp.bfloat16)
    return (
        weight_grad,
        jnp.sum(scaled, 0),
        hidden_grad,
        jnp.sum(hidden_grad.astype(jnp.float32), 0),
    )


def panel_terms(word_block, column_block, grad_block):
    matrix, inverse = unpack(word_block)
    rows_one = grad_block.shape[1]
    gathered = (
        jnp.einsum("brdn,bcn->brdc", matrix, column_block, preferred_element_type=jnp.float32)
        * inverse[..., None]
    ).astype(jnp.bfloat16)
    panel_rel = jnp.einsum(
        "brdc,bdh->rch", gathered, grad_block, preferred_element_type=jnp.float32
    )
    panel_self = jnp.einsum(
        "bcd,bdh->ch", column_block[:, :, :rows_one], grad_block, preferred_element_type=jnp.float32
    )
    return jnp.concatenate([panel_self[None], panel_rel], 0)


def on_device(features, adjacency_one, pre_hidden, adjacency_two, weight_two, out_grad):
    seed_count = out_grad.shape[2]
    factor = float(seed_count * lax.axis_size(FEAT) * lax.axis_size("rep")) ** (-0.5)
    weight_grad, bias_two, hidden_grad, bias_one = upper_layer(
        pre_hidden[0, 0], adjacency_two[0, 0], out_grad[0, 0], weight_two, factor
    )
    feature_local = features[0]
    adj_local = adjacency_one[0]
    col_width = feature_local.shape[1]
    hidden_width = hidden_grad.shape[1]
    relations = adj_local.shape[1]
    initial = jnp.zeros((relations + 1, col_width, hidden_width), jnp.float32)
    piece = gather_axes(hidden_grad[None], FEAT, (2, 0, 1), 0)
    piece_rows = piece.shape[0]
    group_size = math.gcd(piece_rows, 8)
    turn_count = piece_rows // group_size
    word_block = adj_local
    word_block = word_block.reshape((turn_count, group_size) + adj_local.shape[1:])
    column_block = feature_local
    column_block = column_block.reshape((turn_count, group_size) + feature_local.shape[1:])
    grad_block = piece.reshape((turn_count, group_size) + piece.shape[1:])

    def one_turn(running, inputs):
        return (running + panel_terms(inputs[0], inputs[1], inputs[2]), None)

    running, unused = lax.scan(one_turn, initial, (word_block, column_block, grad_block))
    grad_w1 = of_everyone(running, "rep")
    grad_w2, grad_b1, grad_b2 = lax.psum((weight_grad, bias_one, bias_two), FEAT_REP)
    return (grad_w1, grad_b1, grad_w2, grad_b2)


def solution(mesh):
    torus = Mesh(
        mesh.devices.reshape(4, 4, 4, mesh.shape["rep"]), ("feat_0", "feat_1", "feat_2", "rep")
    )
    placed = (
        P("rep", None, FEAT, None),
        P("rep", None, None, None, None),
        P("rep", FEAT, None, None),
        P("rep", FEAT, None, None, None),
        P(),
        P("rep", FEAT, None, None),
    )
    return jax.shard_map(
        on_device,
        mesh=torus,
        in_specs=placed,
        out_specs=(P(None, FEAT, None), P(), P(), P()),
        check_vma=False,
    )
```

profile of v0, /device:TPU:1, one launch (start us, length us, event | category | flops | bytes accessed | tf_op | source)
XLA Modules:
  0.0 494.7 jit_solution(360926030646773313)
XLA Ops:
  13.6 16.8 %all-gather = bf16[1024,256]{1,0:T(8,128)(2,1)} all-gather(bf16[256,256]{1,0:T(8,128)(2,1)S(1)} %get-tuple-element.80), channel_id=2, replica_groups=mesh['feat_0'=4,'feat_1'=4,'feat_2'=4,'rep'=4] {'feat_2'}, dimensions={0}, use_global_device_ids=true | all-gather | bytes 655360 | tf_op jit(solution)/shard_map/all_gather | solution.py:22
  30.5 36.3 %all-gather.6.cloned.1.call-done = bf16[16,1,256,256]{3,2,1,0:T(8,128)(2,1)} async-done(((bf16[4,1,256,256]{3,2,1,0:T(8,128)(2,1)}), bf16[16,1,256,256]{3,2,1,0:T(8,128)(2,1)}) %all-gather.6.cloned.1.call-update) | async-done | bytes 2097168 | tf_op jit(solution)/shard_map/all_gather | solution.py:22
  71.7 83.4 %all-gather.8.cloned.1.call-done = bf16[16,4,1,256,256]{4,3,2,1,0:T(8,128)(2,1)} async-done(((bf16[4,4,1,256,256]{4,3,2,1,0:T(8,128)(2,1)}), bf16[16,4,1,256,256]{4,3,2,1,0:T(8,128)(2,1)}) %all-gather.8.cloned.1.call-update) | async-done | bytes 8388624 | tf_op jit(solution)/shard_map/all_gather | solution.py:22
  155.1 7.7 %copy.30 = bf16[4,4,4,1,256,256]{5,4,2,1,0,3:T(8,128)(2,1)} copy(bf16[4,4,4,1,256,256]{5,4,2,0,1,3:T(8,128)(2,1)} %bitcast.128) | data formatting | bytes 16777216 | tf_op jit(solution)/shard_map/transpose | solution.py:25
  162.9 235.7 %while.11 = (s32[]{:T(128)}, f32[6,16,256]{2,1,0:T(8,128)S(1)}, bf16[8,8,16,512]{3,2,1,0:T(8,128)(2,1)}, bf16[8,8,256,256]{3,2,1,0:T(8,128)(2,1)}, s32[8,8,5,16,512]{4,3,2,1,0:T(8,128)}, /*index=5*/s32[]{:T(128)}, s32[]{:T(128)}) while((s32[]{:T(128)}, f32[6,16,256]{2,1,0:T(8,128)S(1)}, bf16[8,8,16,512]{3,2,1,0:T(8,128)(2,1)}, ...), condition=%wide.region_3.4_spmd.clone, body=%wide.region_1.3_spmd.clone.sunk | while | flops 300314624 | bytes 29414504 | solution.py:124
  166.8 10.9 %and_reduce_fusion.2 = s32[8,5,16,16]{3,2,0,1:T(8,128)S(1)} fusion(s32[8,5,16,512]{3,2,0,1:T(8,128)S(1)} %copy_bitcast_fusion.2), kind=kLoop, calls=%fused_computation.3.clone.1 | loop fusion | flops 15718400 | bytes 1351680 | tf_op jit(solution)/shard_map/while/body/eval_jaxpr/reduce_sum | solution.py:46
  177.9 7.0 %fusion.76 = bf16[8,5,256,512]{3,2,0,1:T(8,128)(2,1)} fusion(s32[256]{0:T(256)S(1)} %shift_right_arithmetic.123, s32[8,5,16,512]{3,2,0,1:T(8,128)S(1)} %copy_bitcast_fusion.2), kind=kLoop, calls=%fused_computation.2.clone.1 | loop fusion | flops 15728640 | bytes 11797504 | tf_op jit(solution)/shard_map/while/body/eval_jaxpr/convert_element_type | solution.py:47
  184.8 7.4 %fusion.77 = f32[5,16,256]{2,1,0:T(8,128)S(1)} fusion(bf16[8,5,256,512]{3,2,0,1:T(8,128)(2,1)} %fusion.76, bf16[8,8,256,256]{3,2,1,0:T(8,128)(2,1)} %get-tuple-element.129, s32[]{:T(128)S(6)} %copy.42, f32[8,5,256]{2,0,1:T(8,128)S(1)} %div.29, bf16[8,8,16,512]{3,2,1,0:T(8,128)(2,1)} %get-tuple-element.128), kind=kOutput, calls=%fused_computation.8.clone.1 | convolution fusion | flops 251985920 | bytes 11789312 | tf_op jit(solution)/shard_map/while/body/eval_jaxpr/brdc,bdh->rch/dot_general | solution.py:90
  196.2 10.9 %and_reduce_fusion.2 = s32[8,5,16,16]{3,2,0,1:T(8,128)S(1)} fusion(s32[8,5,16,512]{3,2,0,1:T(8,128)S(1)} %copy_bitcast_fusion.2), kind=kLoop, calls=%fused_computation.3.clone.1 | loop fusion | flops 15718400 | bytes 1351680 | tf_op jit(solution)/shard_map/while/body/eval_jaxpr/reduce_sum | solution.py:46
  214.3 7.4 %fusion.77 = f32[5,16,256]{2,1,0:T(8,128)S(1)} fusion(bf16[8,5,256,512]{3,2,0,1:T(8,128)(2,1)} %fusion.76, bf16[8,8,256,256]{3,2,1,0:T(8,128)(2,1)} %get-tuple-element.129, s32[]{:T(128)S(6)} %copy.42, f32[8,5,256]{2,0,1:T(8,128)S(1)} %div.29, bf16[8,8,16,512]{3,2,1,0:T(8,128)(2,1)} %get-tuple-element.128), kind=kOutput, calls=%fused_computation.8.clone.1 | convolution fusion | flops 251985920 | bytes 11789312 | tf_op jit(solution)/shard_map/while/body/eval_jaxpr/brdc,bdh->rch/dot_general | solution.py:90
  225.7 10.9 %and_reduce_fusion.2 = s32[8,5,16,16]{3,2,0,1:T(8,128)S(1)} fusion(s32[8,5,16,512]{3,2,0,1:T(8,128)S(1)} %copy_bitcast_fusion.2), kind=kLoop, calls=%fused_computation.3.clone.1 | loop fusion | flops 15718400 | bytes 1351680 | tf_op jit(solution)/shard_map/while/body/eval_jaxpr/reduce_sum | solution.py:46
  243.7 7.5 %fusion.77 = f32[5,16,256]{2,1,0:T(8,128)S(1)} fusion(bf16[8,5,256,512]{3,2,0,1:T(8,128)(2,1)} %fusion.76, bf16[8,8,256,256]{3,2,1,0:T(8,128)(2,1)} %get-tuple-element.129, s32[]{:T(128)S(6)} %copy.42, f32[8,5,256]{2,0,1:T(8,128)S(1)} %div.29, bf16[8,8,16,512]{3,2,1,0:T(8,128)(2,1)} %get-tuple-element.128), kind=kOutput, calls=%fused_computation.8.clone.1 | convolution fusion | flops 251985920 | bytes 11789312 | tf_op jit(solution)/shard_map/while/body/eval_jaxpr/brdc,bdh->rch/dot_general | solution.py:90
  255.2 10.9 %and_reduce_fusion.2 = s32[8,5,16,16]{3,2,0,1:T(8,128)S(1)} fusion(s32[8,5,16,512]{3,2,0,1:T(8,128)S(1)} %copy_bitcast_fusion.2), kind=kLoop, calls=%fused_computation.3.clone.1 | loop fusion | flops 15718400 | bytes 1351680 | tf_op jit(solution)/shard_map/while/body/eval_jaxpr/reduce_sum | solution.py:46
  273.2 7.4 %fusion.77 = f32[5,16,256]{2,1,0:T(8,128)S(1)} fusion(bf16[8,5,256,512]{3,2,0,1:T(8,128)(2,1)} %fusion.76, bf16[8,8,256,256]{3,2,1,0:T(8,128)(2,1)} %get-tuple-element.129, s32[]{:T(128)S(6)} %copy.42, f32[8,5,256]{2,0,1:T(8,128)S(1)} %div.29, bf16[8,8,16,512]{3,2,1,0:T(8,128)(2,1)} %get-tuple-element.128), kind=kOutput, calls=%fused_computation.8.clone.1 | convolution fusion | flops 251985920 | bytes 11789312 | tf_op jit(solution)/shard_map/while/body/eval_jaxpr/brdc,bdh->rch/dot_general | solution.py:90
  284.6 10.9 %and_reduce_fusion.2 = s32[8,5,16,16]{3,2,0,1:T(8,128)S(1)} fusion(s32[8,5,16,512]{3,2,0,1:T(8,128)S(1)} %copy_bitcast_fusion.2), kind=kLoop, calls=%fused_computation.3.clone.1 | loop fusion | flops 15718400 | bytes 1351680 | tf_op jit(solution)/shard_map/while/body/eval_jaxpr/reduce_sum | solution.py:46
  302.7 7.4 %fusion.77 = f32[5,16,256]{2,1,0:T(8,128)S(1)} fusion(bf16[8,5,256,512]{3,2,0,1:T(8,128)(2,1)} %fusion.76, bf16[8,8,256,256]{3,2,1,0:T(8,128)(2,1)} %get-tuple-element.129, s32[]{:T(128)S(6)} %copy.42, f32[8,5,256]{2,0,1:T(8,128)S(1)} %div.29, bf16[8,8,16,512]{3,2,1,0:T(8,128)(2,1)} %get-tuple-element.128), kind=kOutput, calls=%fused_computation.8.clone.1 | convolution fusion | flops 251985920 | bytes 11789312 | tf_op jit(solution)/shard_map/while/body/eval_jaxpr/brdc,bdh->rch/dot_general | solution.py:90
  314.0 10.9 %and_reduce_fusion.2 = s32[8,5,16,16]{3,2,0,1:T(8,128)S(1)} fusion(s32[8,5,16,512]{3,2,0,1:T(8,128)S(1)} %copy_bitcast_fusion.2), kind=kLoop, calls=%fused_computation.3.clone.1 | loop fusion | flops 15718400 | bytes 1351680 | tf_op jit(solution)/shard_map/while/body/eval_jaxpr/reduce_sum | solution.py:46
  332.1 7.5 %fusion.77 = f32[5,16,256]{2,1,0:T(8,128)S(1)} fusion(bf16[8,5,256,512]{3,2,0,1:T(8,128)(2,1)} %fusion.76, bf16[8,8,256,256]{3,2,1,0:T(8,128)(2,1)} %get-tuple-element.129, s32[]{:T(128)S(6)} %copy.42, f32[8,5,256]{2,0,1:T(8,128)S(1)} %div.29, bf16[8,8,16,512]{3,2,1,0:T(8,128)(2,1)} %get-tuple-element.128), kind=kOutput, calls=%fused_computation.8.clone.1 | convolution fusion | flops 251985920 | bytes 11789312 | tf_op jit(solution)/shard_map/while/body/eval_jaxpr/brdc,bdh->rch/dot_general | solution.py:90
  343.6 10.9 %and_reduce_fusion.2 = s32[8,5,16,16]{3,2,0,1:T(8,128)S(1)} fusion(s32[8,5,16,512]{3,2,0,1:T(8,128)S(1)} %copy_bitcast_fusion.2), kind=kLoop, calls=%fused_computation.3.clone.1 | loop fusion | flops 15718400 | bytes 1351680 | tf_op jit(solution)/shard_map/while/body/eval_jaxpr/reduce_sum | solution.py:46
  361.7 7.4 %fusion.77 = f32[5,16,256]{2,1,0:T(8,128)S(1)} fusion(bf16[8,5,256,512]{3,2,0,1:T(8,128)(2,1)} %fusion.76, bf16[8,8,256,256]{3,2,1,0:T(8,128)(2,1)} %get-tuple-element.129, s32[]{:T(128)S(6)} %copy.42, f32[8,5,256]{2,0,1:T(8,128)S(1)} %div.29, bf16[8,8,16,512]{3,2,1,0:T(8,128)(2,1)} %get-tuple-element.128), kind=kOutput, calls=%fused_computation.8.clone.1 | convolution fusion | flops 251985920 | bytes 11789312 | tf_op jit(solution)/shard_map/while/body/eval_jaxpr/brdc,bdh->rch/dot_general | solution.py:90
  373.1 10.9 %and_reduce_fusion.2 = s32[8,5,16,16]{3,2,0,1:T(8,128)S(1)} fusion(s32[8,5,16,512]{3,2,0,1:T(8,128)S(1)} %copy_bitcast_fusion.2), kind=kLoop, calls=%fused_computation.3.clone.1 | loop fusion | flops 15718400 | bytes 1351680 | tf_op jit(solution)/shard_map/while/body/eval_jaxpr/reduce_sum | solution.py:46
  391.1 7.4 %fusion.77 = f32[5,16,256]{2,1,0:T(8,128)S(1)} fusion(bf16[8,5,256,512]{3,2,0,1:T(8,128)(2,1)} %fusion.76, bf16[8,8,256,256]{3,2,1,0:T(8,128)(2,1)} %get-tuple-element.129, s32[]{:T(128)S(6)} %copy.42, f32[8,5,256]{2,0,1:T(8,128)S(1)} %div.29, bf16[8,8,16,512]{3,2,1,0:T(8,128)(2,1)} %get-tuple-element.128), kind=kOutput, calls=%fused_computation.8.clone.1 | convolution fusion | flops 251985920 | bytes 11789312 | tf_op jit(solution)/shard_map/while/body/eval_jaxpr/brdc,bdh->rch/dot_general | solution.py:90
  399.3 7.8 %all-to-all-start = ((f32[4,6,16,256]{3,2,1,0:T(8,128)}), f32[4,6,16,256]{3,2,1,0:T(8,128)S(1)}, u32[]{:S(2)}, u32[]{:S(2)}) async-start(f32[4,6,16,256]{3,2,1,0:T(8,128)} %broadcast_in_dim.23), calls=%async_computation | async-start | bytes 786432 | tf_op jit(solution)/shard_map/all_to_all | solution.py:35
  407.2 76.6 %all-reduce.1 = (f32[256]{0:T(256)}, f32[256]{0:T(256)}) all-reduce(f32[256]{0:T(256)S(1)} %get-tuple-element.79, f32[256]{0:T(256)S(1)} %fusion.40), channel_id=1, replica_groups=mesh['feat_0'=4,'feat_1'=4,'feat_2'=4,'rep'=4] {'feat_0','feat_1','feat_..., use_global_device_ids=true, to_apply=%region_6.7 | all-reduce | flops 512 | bytes 4096 | tf_op jit(solution)/shard_map/psum | solution.py:126
  (98 shorter events, 96.8 us)
Async XLA Ops:
  8.0 58.8 %all-gather.6.cloned.1.call-start = ((), (), s32[]{:S(2)}) async-start(), calls=%async_computation.2 | async-start | bytes 2621440 | tf_op jit(solution)/shard_map/all_gather | solution.py:22
  30.4 124.7 %all-gather.8.cloned.1.call-start = ((), (), s32[]{:S(2)}) async-start(), calls=%async_computation.3 | async-start | bytes 10485760 | tf_op jit(solution)/shard_map/all_gather | solution.py:22
  66.8 417.7 %all-reduce.4.cloned.1.call-start = ((), (), s32[]{:S(2)}) async-start(), calls=%async_computation.1 | async-start | bytes 3145728 | tf_op jit(solution)/shard_map/psum | solution.py:126
  162.9 244.3 %copy-start = (bf16[1,1,128,256]{3,2,1,0:T(8,128)(2,1)S(1)}, bf16[1,1,128,256]{3,2,1,0:T(8,128)(2,1)}, u32[]{:S(2)}) copy-start(bf16[1,1,128,256]{3,2,1,0:T(8,128)(2,1)} %param.13) | copy-start | bytes 196612
  399.3 84.5 %all-to-all-start = ((f32[4,6,16,256]{3,2,1,0:T(8,128)}), f32[4,6,16,256]{3,2,1,0:T(8,128)S(1)}, u32[]{:S(2)}, u32[]{:S(2)}) async-start(f32[4,6,16,256]{3,2,1,0:T(8,128)} %broadcast_in_dim.23), calls=%async_computation | async-start | bytes 786432 | tf_op jit(solution)/shard_map/all_to_all | solution.py:35
Sparse Core Ops, SparseCore 0:
  30.5 36.1 all-gather.5
  68.6 86.5 all-gather.7
Sparse Core Ops, SparseCore 1:
  73.2 308.0 all-reduce.3
where the time goes:
time: 496 us; the launch traced here: 495 us
  other arithmetic  149 us (30%)
  waiting for transfers between devices  120 us (24%)
  blocking collectives  93.4 us (19%)
  matrix products  76.7 us (15%)
  local copies, waits for them, and re-layouts  32.2 us (6%)
  between operations  15.6 us (3%)
  starting transfers between devices  7.95 us (2%)
    all_gather x2, waiting for transfers between devices, all_blocks(): tiles = lax.all_gather(tiles, axes[k])  120 us
    reduce_sum x8, other arithmetic, unpack(): degree = jnp.sum(dense, axis=-1).astype(jnp.float32)  86.9 us
    psum x1, blocking collectives, on_device(): lax.psum((weight_grad, bias_one, bias_two), FEAT_REP)  76.6 us
    dot_general x8, matrix products, panel_terms(): jnp.einsum('brdc,bdh->rch', gathered, grad_block, preferred_element_type=...  59.3 us
    convert_element_type x10, other arithmetic, unpack(): return (dense.astype(jnp.bfloat16), 1.0 / jnp.maximum(degree, 1.0))  58.2 us
    all_gather x1, blocking collectives, all_blocks(): tiles = lax.all_gather(tiles, axes[k])  16.8 us
    shift_right_arithmetic x26, local copies, waits for them, and re-layouts, unpack(): jnp.right_shift(packed[..., None, :], shifts[:, None])  12.2 us
    dot_general x8, matrix products, panel_terms(): jnp.einsum('bcd,bdh->ch', column_block[:, :, :rows_one], grad_block, pref...  11.8 us
  transfers between devices with their start and end apart: 4, of which 2 were waited for; matrix products, arithmetic and copies ran while one was open for 50% of the time, Pallas kernels for 0%

commit v1 on v0

v1 whole, which is shorter than its diff:
```python
import functools

import jax
import jax.numpy as jnp
from jax import lax
from jax.experimental import pallas as pl
from jax.experimental.pallas import tpu as pltpu
from jax.sharding import Mesh
from jax.sharding import PartitionSpec as P

MESH = pl.DeviceIdType.MESH
AXES = ("y", "x", "z", "g", "c")
FEAT = ("y", "x", "z")
REP = ("g", "c")
BF16 = jnp.bfloat16
F32 = jnp.float32
NN = (((1,), (0,)), ((), ()))
NT = (((1,), (1,)), ((), ()))
TN = (((0,), (0,)), ((), ()))


def mm(a, b, dims):
    return lax.dot_general(a, b, dims, preferred_element_type=F32)


def local(src, dst, sem):
    return pltpu.make_async_copy(src, dst, sem)


def spread_bits(words, r, out, rows, width):
    shift = lax.broadcasted_iota(jnp.int32, (16, width), 0)
    for w in range(rows // 16):
        word = jnp.broadcast_to(words[r, pl.ds(w, 1), :], (16, width))
        bits = lax.bitwise_and(lax.shift_right_logical(word, shift), 1)
        out[r, pl.ds(16 * w, 16), :] = bits.astype(F32).astype(BF16)


def kernel(
    dims,
    factor,
    feat,
    adj1,
    pre_any,
    adj2,
    w2_any,
    og_any,
    out1,
    out2,
    outb,
    pre,
    words2,
    w2,
    og,
    words1,
    dense2,
    dense1,
    c1,
    rx,
    hgbuf,
    total,
    acc,
    wg,
    cxs2,
    cxr2,
    s2,
    r2,
    zbuf,
    agbuf,
    agp,
    cxs1,
    cxr1,
    s1,
    r1,
    zhs,
    zhr,
    d1s,
    d1r,
    loc_sem,
    own_sem,
    xs_sem,
    xr_sem,
    hs_sem,
    hr_sem,
    px_sem,
):
    Y, X, Z, G, C = dims
    NP, ZZ = Y * X, Z * G
    y, x, z, g, c = (lax.axis_index(a) for a in AXES)
    me = y * X + x
    zabs = g * Z + z
    relations = words1.shape[0] // Z
    half = (relations + 1) // C
    cw = feat.shape[2]
    h = w2.shape[1]
    hc = h // NP
    seeds = og.shape[0]

    def plane(k, sign):
        yy = lax.rem(y + sign * lax.div(k, X) + Y, Y)
        xx = lax.rem(x + sign * lax.rem(k, X) + X, X)
        return yy * X + xx, (yy, xx, z, g, c)

    def column(zz):
        return (y, x, lax.rem(zz, Z), lax.div(zz, Z), c)

    partner = (y, x, z, g, 1 - c)
    across = (y, x, z, 1 - g, c)

    def remote(src, dst, send, recv, device):
        return pltpu.make_async_remote_copy(
            src_ref=src, dst_ref=dst, send_sem=send, recv_sem=recv, device_id=device, device_id_type=MESH
        )

    barrier = pltpu.get_barrier_semaphore()

    def greet_plane(k, carry):
        pl.semaphore_signal(barrier, inc=1, device_id=plane(k, 1)[1], device_id_type=MESH)
        return carry

    def greet_column(k, carry):
        pl.semaphore_signal(barrier, inc=1, device_id=column(lax.rem(zabs + k, ZZ)), device_id_type=MESH)
        return carry

    lax.fori_loop(1, NP, greet_plane, 0)
    lax.fori_loop(1, ZZ, greet_column, 0)
    pl.semaphore_signal(barrier, inc=1, device_id=partner, device_id_type=MESH)

    base = me * Z
    loads = [
        local(adj2.at[0, 0], words2, loc_sem.at[0]),
        local(pre_any.at[0, 0], pre, loc_sem.at[1]),
        local(og_any.at[0, 0], og, loc_sem.at[2]),
        local(w2_any, w2, loc_sem.at[3]),
    ]
    for q in range(Z):
        loads.append(
            local(adj1.at[0, base + q], words1.at[pl.ds(q * relations, relations)], loc_sem.at[4 + q])
        )
    for load in loads:
        load.start()

    loads[0].wait()
    for r in range(relations):
        spread_bits(words2, r, dense2, seeds, h)
    pl.semaphore_wait(barrier, NP + ZZ - 1)

    for i in range(Z):
        m = lax.rem(z + i, Z)
        local(feat.at[0, base + m], rx.at[m, pl.ds(0, cw), :], own_sem.at[i]).start()

        def send_features(k, carry):
            other, device = plane(k, 1)
            remote(
                feat.at[0, other * Z + m],
                rx.at[m, pl.ds(pl.multiple_of(k * cw, cw), cw), :],
                xs_sem.at[i],
                xr_sem.at[i],
                device,
            ).start()
            return carry

        lax.fori_loop(1, NP, send_features, 0)

    for load in loads[1:4]:
        load.wait()
    hidden = jnp.maximum(pre[...], 0)
    scaled = og[...].astype(F32) * factor
    low = scaled.astype(BF16)
    ones = jnp.ones((h, h), BF16)
    wg[0] = mm(hidden[:seeds], low, TN)
    total[...] = jnp.zeros_like(total)
    total[pl.ds(0, seeds), :] = mm(low, w2[0], NT)
    for r in range(relations):
        dense = dense2[r]
        inverse = 1.0 / jnp.maximum(mm(dense, ones, NN), 1.0)
        mixed = (mm(dense, hidden, NN) * inverse).astype(BF16)
        wg[r + 1] = mm(mixed, low, TN)
        backed = (mm(low, w2[r + 1], NT) * inverse).astype(BF16)
        total[...] += mm(dense, backed, TN)
    grad = jnp.where(pre[...] > 0, total[...], 0.0).astype(BF16)
    hgbuf[z] = grad
    row = lax.broadcasted_iota(jnp.int32, (8, h), 0)
    bias_one = jnp.sum(grad.astype(F32), axis=0, keepdims=True)
    bias_two = jnp.sum(scaled, axis=0, keepdims=True)
    first = c == 0
    bias_keep = jnp.where(row == 0, jnp.where(first, bias_one, bias_two), 0.0)
    bias_give = jnp.where(row == 0, jnp.where(first, bias_two, bias_one), 0.0)
    for q in range(half):
        cxs2[pl.ds(q * h, h), :] = wg[(1 - c) * half + q].astype(BF16)
    cxs2[pl.ds(half * h, 8), :] = bias_give.astype(BF16)
    swap2 = remote(cxs2, cxr2, px_sem.at[0], px_sem.at[1], partner)
    swap2.start()

    def give_grad(k):
        other = lax.rem(z + Z - k, Z)
        return remote(
            hgbuf.at[z], hgbuf.at[z], hs_sem.at[k], hr_sem.at[k], (y, x, other, g, c)
        )

    for k in range(1, Z):
        give_grad(k).start()

    for load in loads[4:]:
        load.wait()
    ones_row = jnp.ones((16, words1.shape[2]), BF16)

    def spread_one(t, carry):
        spread_bits(words1, t, dense1, 16 * words1.shape[1], words1.shape[2])
        count = mm(ones_row, dense1[t], NT)
        c1[t] = 1.0 / jnp.maximum(count[:8], 1.0)
        return carry

    lax.fori_loop(0, Z * relations, spread_one, 0)

    swap2.wait_recv()
    for q in range(half):
        both = wg[c * half + q] + cxr2[pl.ds(q * h, h), :].astype(F32)
        s2[:, pl.ds(q * hc, hc), :] = both.astype(BF16).reshape(NP, hc, h)
    bias = (bias_keep + cxr2[pl.ds(half * h, 8), :].astype(F32)).astype(BF16)
    s2[:, pl.ds(half * hc, 8), :] = jnp.broadcast_to(bias[None], (NP, 8, h))

    def send_second(k, carry):
        other, device = plane(k, 1)
        remote(s2.at[other], r2.at[k], px_sem.at[2], px_sem.at[3], device).start()
        return carry

    lax.fori_loop(1, NP, send_second, 0)

    acc[...] = jnp.zeros_like(acc)
    for i in range(Z):
        m = lax.rem(z + i, Z)
        if i:
            give_grad(i).wait_recv()
        local(feat.at[0, base + m], rx.at[m, pl.ds(0, cw), :], own_sem.at[i]).wait()
        arrived = rx.at[m, pl.ds(cw, (NP - 1) * cw), :]
        local(arrived, arrived, xr_sem.at[i]).wait()
        columns = rx[m]
        grad_m = hgbuf[m]
        acc[0] += mm(columns[:, : grad_m.shape[0]], grad_m, NN)

        def one_relation(r, carry):
            t = m * relations + r
            gathered = (mm(columns, dense1[t], NT) * c1[t][:1]).astype(BF16)
            acc[r + 1] += mm(gathered, grad_m, NN)
            return carry

        lax.fori_loop(0, relations, one_relation, 0)

    for q in range(half):
        cxs1[q] = acc[(1 - c) * half + q].astype(BF16)
    swap1 = remote(cxs1, cxr1, px_sem.at[4], px_sem.at[5], partner)
    swap1.start()

    second_in = r2.at[pl.ds(1, NP - 1)]
    local(second_in, second_in, px_sem.at[3]).wait()
    summed = s2[me].astype(F32)
    for k in range(1, NP):
        summed += r2[k].astype(F32)
    zbuf[zabs] = summed.astype(BF16)

    def send_column(k, carry):
        remote(
            zbuf.at[zabs], zbuf.at[zabs], px_sem.at[6], px_sem.at[7], column(lax.rem(zabs + k, ZZ))
        ).start()
        return carry

    lax.fori_loop(1, ZZ, send_column, 0)

    swap1.wait_recv()
    for q in range(half):
        both = acc[c * half + q] + cxr1[q].astype(F32)
        s1[:, pl.ds(q * cw, cw), :] = both.astype(BF16).reshape(NP, cw, h)

    def send_first(k, carry):
        other, device = plane(k, -1)
        remote(s1.at[k], r1.at[k], px_sem.at[8], px_sem.at[9], device).start()
        return carry

    lax.fori_loop(1, NP, send_first, 0)

    column_in = zbuf.at[pl.ds(0, ZZ - 1)]
    local(column_in, column_in, px_sem.at[7]).wait()
    summed = zbuf[0].astype(F32)
    for k in range(1, ZZ):
        summed += zbuf[k].astype(F32)
    agbuf[me] = summed.astype(BF16)

    def send_everyone(k, carry):
        other, device = plane(k, 1)
        remote(agbuf.at[me], agbuf.at[me], px_sem.at[10], px_sem.at[11], device).start()
        return carry

    lax.fori_loop(1, NP, send_everyone, 0)

    first_in = r1.at[pl.ds(1, NP - 1)]
    local(first_in, first_in, px_sem.at[9]).wait()
    summed = s1[0].astype(F32)
    for k in range(1, NP):
        summed += r1[k].astype(F32)
    zhs[...] = summed.astype(BF16)
    cross = remote(zhs, zhr, px_sem.at[12], px_sem.at[13], across)
    cross.start()

    everyone_in = agbuf.at[pl.ds(0, NP - 1)]
    local(everyone_in, everyone_in, px_sem.at[11]).wait()
    swap3 = remote(agbuf, agp, px_sem.at[14], px_sem.at[15], partner)
    swap3.start()
    for q in range(half):
        out2[c * half + q] = agbuf[:, pl.ds(q * hc, hc), :].astype(F32).reshape(h, h)

    cross.wait_recv()
    final = (zhs[...].astype(F32) + zhr[...].astype(F32)).reshape(half, cw, h)
    d1s[...] = final
    swap4 = remote(d1s, d1r, px_sem.at[16], px_sem.at[17], partner)
    swap4.start()
    out1[pl.ds(c * half, half)] = final

    swap3.wait_recv()
    for q in range(half):
        out2[(1 - c) * half + q] = agp[:, pl.ds(q * hc, hc), :].astype(F32).reshape(h, h)
    kept = agbuf[0, pl.ds(half * hc, 8), :].astype(F32)[:1]
    given = agp[0, pl.ds(half * hc, 8), :].astype(F32)[:1]
    outb[...] = jnp.where(row == c, kept, given)
    swap4.wait_recv()
    out1[pl.ds((1 - c) * half, half)] = d1r[...]

    for i in range(Z):
        sent = feat.at[0, pl.ds(0, NP - 1)]
        local(sent, sent, xs_sem.at[i]).wait()
    for k in range(1, Z):
        give_grad(k).wait_send()
    for swap in (swap2, swap1, cross, swap3, swap4):
        swap.wait_send()
    local(second_in, second_in, px_sem.at[2]).wait()
    local(column_in, column_in, px_sem.at[6]).wait()
    local(first_in, first_in, px_sem.at[8]).wait()
    local(everyone_in, everyone_in, px_sem.at[10]).wait()


def on_device(dims, features, adjacency_one, pre_hidden, adjacency_two, weight_two, out_grad):
    Y, X, Z, G, C = dims
    NP, ZZ = Y * X, Z * G
    cw, nb = features.shape[2:]
    relations, word_rows = adjacency_one.shape[2:4]
    dst, h = pre_hidden.shape[2:]
    seeds = out_grad.shape[2]
    half = (relations + 1) // C
    hc = h // NP
    rows2 = half * hc + 8
    factor = float(seeds * NP * ZZ * C) ** (-0.5)
    vmem = pltpu.VMEM
    any_spec = pl.BlockSpec(memory_space=pl.ANY)
    vmem_spec = pl.BlockSpec(memory_space=pltpu.VMEM)
    dma = pltpu.SemaphoreType.DMA
    out1, out2, outb = pl.pallas_call(
        functools.partial(kernel, dims, factor),
        name="graph_grads",
        out_shape=(
            jax.ShapeDtypeStruct((relations + 1, cw, h), F32),
            jax.ShapeDtypeStruct((relations + 1, h, h), F32),
            jax.ShapeDtypeStruct((8, h), F32),
        ),
        in_specs=[any_spec] * 6,
        out_specs=(vmem_spec,) * 3,
        scratch_shapes=[
            vmem((dst, h), BF16),
            vmem(adjacency_two.shape[2:], jnp.int32),
            vmem(weight_two.shape, BF16),
            vmem((seeds, h), BF16),
            vmem((Z * relations, word_rows, nb), jnp.int32),
            vmem((relations, seeds, dst), BF16),
            vmem((Z * relations, dst, nb), BF16),
            vmem((Z * relations, 8, dst), F32),
            vmem((Z, NP * cw, nb), BF16),
            vmem((Z, dst, h), BF16),
            vmem((dst, h), F32),
            vmem((relations + 1, NP * cw, h), F32),
            vmem((relations + 1, h, h), F32),
            vmem((half * h + 8, h), BF16),
            vmem((half * h + 8, h), BF16),
            vmem((NP, rows2, h), BF16),
            vmem((NP, rows2, h), BF16),
            vmem((ZZ, rows2, h), BF16),
            vmem((NP, rows2, h), BF16),
            vmem((NP, rows2, h), BF16),
            vmem((half, NP * cw, h), BF16),
            vmem((half, NP * cw, h), BF16),
            vmem((NP, half * cw, h), BF16),
            vmem((NP, half * cw, h), BF16),
            vmem((half * cw, h), BF16),
            vmem((half * cw, h), BF16),
            vmem((half, cw, h), F32),
            vmem((half, cw, h), F32),
            dma((4 + Z,)),
            dma((Z,)),
            dma((Z,)),
            dma((Z,)),
            dma((Z,)),
            dma((Z,)),
            dma((18,)),
        ],
        compiler_params=pltpu.CompilerParams(
            collective_id=0, has_side_effects=True, vmem_limit_bytes=48 * 2**20
        ),
    )(features, adjacency_one, pre_hidden, adjacency_two, weight_two, out_grad)
    return out1, outb[0], out2, outb[1]


def build(devices, dims):
    torus = Mesh(devices.reshape(dims), AXES)
    placed = (
        P(REP, None, FEAT, None),
        P(REP, None, None, None, None),
        P(REP, FEAT, None, None),
        P(REP, FEAT, None, None, None),
        P(),
        P(REP, FEAT, None, None),
    )
    return jax.shard_map(
        functools.partial(on_device, dims),
        mesh=torus,
        in_specs=placed,
        out_specs=(P(None, FEAT, None), P(), P(), P()),
        check_vma=False,
    )


def solution(mesh):
    dims = (4, 4, mesh.shape["feat"] // 16, mesh.shape["rep"] // 2, 2)
    return build(mesh.devices, dims)
```

time: 496 us -> 56 us (0.11)
  other arithmetic: 149 us -> 0 us
  waiting for transfers between devices: 120 us -> 0 us
  blocking collectives: 93.4 us -> 0 us
  matrix products: 76.7 us -> 0 us
  Pallas kernels: 0 us -> 47.9 us
  local copies, waits for them, and re-layouts: 32.2 us -> 7.22 us
  between operations: 15.6 us -> 0.65 us
  starting transfers between devices: 7.95 us -> 0 us
    all_gather x2 -> x0, waiting for transfers between devices: 120 us -> none  [all_blocks(): tiles = lax.all_gather(tiles, axes[k])]
    reduce_sum x10 -> x0, other arithmetic: 87.6 us -> none  [the longest x8 86.9 us: unpack(): degree = jnp.sum(dense, axis=-1).astype(jnp.float32)]
    dot_general x20 -> x0, matrix products: 76.7 us -> none  [the longest x8 59.3 us: panel_terms(): jnp.einsum('brdc,bdh->rch', gathered, grad_block, preferred_element_type=...]
    psum x1 -> x0, blocking collectives: 76.6 us -> none  [on_device(): lax.psum((weight_grad, bias_one, bias_two), FEAT_REP)]
    convert_element_type x10 -> x0, other arithmetic: 58.2 us -> none  [unpack(): return (dense.astype(jnp.bfloat16), 1.0 / jnp.maximum(degree, 1.0))]
    pallas_call x0 -> x1, Pallas kernels: none -> 47.9 us  [on_device(): pl.pallas_call(functools.partial(kernel, dims, factor), name='graph_grads...]
    all_gather x1 -> x0, blocking collectives: 16.8 us -> none  [all_blocks(): tiles = lax.all_gather(tiles, axes[k])]
    shift_right_arithmetic x26 -> x0, local copies, waits for them, and re-layouts: 12.2 us -> none  [unpack(): jnp.right_shift(packed[..., None, :], shifts[:, None])]
  transfers between devices with their start and end apart: 4 -> 0, of which waited for: 2 -> 0; matrix products, arithmetic and copies ran while one was open for 50% -> 0% of each run, Pallas kernels for 0% -> 0%
where the time goes in v1:
time: 56 us; the launch traced here: 55.8 us
  Pallas kernels  47.9 us (86%)
  local copies, waits for them, and re-layouts  7.22 us (13%)
  between operations  0.65 us (1%)
    pallas_call x1, Pallas kernels, on_device(): pl.pallas_call(functools.partial(kernel, dims, factor), name='graph_grads...  47.9 us
    unnamed x12, local copies, waits for them, and re-layouts  6.65 us

profile of v1, /device:TPU:1, one launch (start us, length us, event | category | flops | bytes accessed | tf_op | source)
XLA Modules:
  0.0 55.8 jit_solution(11863569614712370655)
XLA Ops:
  0.6 0.0 copy-start
  0.6 1.2 %copy-done = bf16[1,64,16,512]{3,2,1,0:T(8,128)(2,1)S(1)} copy-done((bf16[1,64,16,512]{3,2,1,0:T(8,128)(2,1)S(1)}, bf16[1,64,16,512]{3,2,1,0:T(8,128)(2,1)}, u32[]{:S(2)}) %copy-start) | copy-done | bytes 1048600
  1.9 0.0 copy-start.1
  1.9 1.1 %copy-done.1 = bf16[6,256,256]{2,1,0:T(8,128)(2,1)S(1)} copy-done((bf16[6,256,256]{2,1,0:T(8,128)(2,1)S(1)}, bf16[6,256,256]{2,1,0:T(8,128)(2,1)}, u32[]{:S(2)}) %copy-start.1) | copy-done | bytes 786456
  3.0 0.0 copy-start.2
  3.0 0.9 %copy-done.2 = bf16[1,1,256,256]{3,2,1,0:T(8,128)(2,1)S(1)} copy-done((bf16[1,1,256,256]{3,2,1,0:T(8,128)(2,1)S(1)}, bf16[1,1,256,256]{3,2,1,0:T(8,128)(2,1)}, u32[]{:S(2)}) %copy-start.2) | copy-done | bytes 131096
  3.9 0.0 copy-start.3
  3.9 0.8 %copy-done.3 = bf16[1,1,128,256]{3,2,1,0:T(8,128)(2,1)S(1)} copy-done((bf16[1,1,128,256]{3,2,1,0:T(8,128)(2,1)S(1)}, bf16[1,1,128,256]{3,2,1,0:T(8,128)(2,1)}, u32[]{:S(2)}) %copy-start.3) | copy-done | bytes 65560
  4.7 0.0 copy-start.4
  4.7 0.8 %copy-done.4 = s32[1,1,5,8,256]{4,3,2,1,0:T(8,128)S(1)} copy-done((s32[1,1,5,8,256]{4,3,2,1,0:T(8,128)S(1)}, s32[1,1,5,8,256]{4,3,2,1,0:T(8,128)}, u32[]{:S(2)}) %copy-start.4) | copy-done | bytes 40984
  5.5 47.9 %graph_grads.1 = (f32[6,16,256]{2,1,0:T(8,128)S(1)}, f32[6,256,256]{2,1,0:T(8,128)S(1)}, f32[8,256]{1,0:T(8,128)S(1)}) custom-call(bf16[1,64,16,512]{3,2,1,0:T(8,128)(2,1)S(1)} %copy-done, s32[1,64,5,16,512]{4,3,2,1,0:T(8,128)} %adj1.1, bf16[1,1,256,256]{3,2,1,0:T(8,128)(2,1)S(1)} %copy-done.2, s32[1,1,5,8,256]{4,3,2,1,0:T(8,128)S(1)} %copy-done.4, ...), custom_call_target="tpu_custom_call" | custom-call | tf_op jit(solution)/shard_map/graph_grads/pallas_call | solution.py:355
  53.4 0.6 %fusion = (f32[1,256]{1,0:T(1,128)}, f32[1,256]{1,0:T(1,128)}) fusion(f32[8,256]{1,0:T(8,128)S(1)} %get-tuple-element.8), kind=kLoop, calls=%fused_computation | loop fusion | bytes 4096 | tf_op jit(solution)/shard_map/slice | solution.py:406
  54.0 0.6 %copy.12 = f32[6,16,256]{2,1,0:T(8,128)} copy(f32[6,16,256]{2,1,0:T(8,128)S(1)} %get-tuple-element.16) | data formatting | bytes 196608
  54.6 1.1 %copy.13 = f32[6,256,256]{2,1,0:T(8,128)} copy(f32[6,256,256]{2,1,0:T(8,128)S(1)} %get-tuple-element.18) | data formatting | bytes 3145728
Async XLA Ops:
  0.6 1.2 %copy-start = (bf16[1,64,16,512]{3,2,1,0:T(8,128)(2,1)S(1)}, bf16[1,64,16,512]{3,2,1,0:T(8,128)(2,1)}, u32[]{:S(2)}) copy-start(bf16[1,64,16,512]{3,2,1,0:T(8,128)(2,1)} %feat.1) | copy-start | bytes 3145732
  1.9 1.1 %copy-start.1 = (bf16[6,256,256]{2,1,0:T(8,128)(2,1)S(1)}, bf16[6,256,256]{2,1,0:T(8,128)(2,1)}, u32[]{:S(2)}) copy-start(bf16[6,256,256]{2,1,0:T(8,128)(2,1)} %w2_any.1) | copy-start | bytes 2359300
  3.0 0.9 %copy-start.2 = (bf16[1,1,256,256]{3,2,1,0:T(8,128)(2,1)S(1)}, bf16[1,1,256,256]{3,2,1,0:T(8,128)(2,1)}, u32[]{:S(2)}) copy-start(bf16[1,1,256,256]{3,2,1,0:T(8,128)(2,1)} %pre_any.1) | copy-start | bytes 393220
  3.9 0.8 %copy-start.3 = (bf16[1,1,128,256]{3,2,1,0:T(8,128)(2,1)S(1)}, bf16[1,1,128,256]{3,2,1,0:T(8,128)(2,1)}, u32[]{:S(2)}) copy-start(bf16[1,1,128,256]{3,2,1,0:T(8,128)(2,1)} %og_any.1) | copy-start | bytes 196612
  4.7 0.8 %copy-start.4 = (s32[1,1,5,8,256]{4,3,2,1,0:T(8,128)S(1)}, s32[1,1,5,8,256]{4,3,2,1,0:T(8,128)}, u32[]{:S(2)}) copy-start(s32[1,1,5,8,256]{4,3,2,1,0:T(8,128)} %adj2.1) | copy-start | bytes 122884

commit v2 on v0

v2 whole, which is shorter than its diff:
```python
import functools
import types

import jax
import jax.numpy as jnp
from jax import lax
from jax.experimental import pallas as pl
from jax.experimental.pallas import tpu as pltpu
from jax.sharding import Mesh
from jax.sharding import PartitionSpec as P

MESH = pl.DeviceIdType.MESH
AXES = ("y", "x", "z", "g", "c")
FEAT = ("y", "x", "z")
REP = ("g", "c")
BF16 = jnp.bfloat16
F32 = jnp.float32
NN = (((1,), (0,)), ((), ()))
NT = (((1,), (1,)), ((), ()))
TN = (((0,), (0,)), ((), ()))
TOP = 16
BIAS = 8
SWAP2, RS2, COL, AG, SWAP3, SWAP1, RS1, CROSS, SWAP4 = range(9)


def mm(a, b, dims):
    return lax.dot_general(a, b, dims, preferred_element_type=F32)


def local(src, dst, sem):
    return pltpu.make_async_copy(src, dst, sem)


def remote(src, dst, send, recv, device):
    return pltpu.make_async_remote_copy(
        src_ref=src, dst_ref=dst, send_sem=send, recv_sem=recv, device_id=device, device_id_type=MESH
    )


def spread_bits(words, r, out, rows, width):
    shift = lax.broadcasted_iota(jnp.int32, (16, width), 0)
    for w in range(rows // 16):
        word = jnp.broadcast_to(words[r, pl.ds(w, 1), :], (16, width))
        bits = lax.bitwise_and(lax.shift_right_logical(word, shift), 1)
        out[r, pl.ds(16 * w, 16), :] = bits.astype(F32).astype(BF16)


def spread_scaled(words, t, out, rows, width):
    mask = lax.shift_left(1, lax.broadcasted_iota(jnp.int32, (16, width), 0))
    for w in range(rows // 16):
        word = jnp.broadcast_to(words[t, pl.ds(w, 1), :], (16, width))
        out[t, pl.ds(16 * w, 16), :] = lax.bitwise_and(word, mask).astype(F32).astype(BF16)


def skip_loop(count, skipped, body):
    def step(t, carry):
        body(t)
        return carry

    lax.fori_loop(0, skipped, step, 0)
    if skipped + 1 < count:
        lax.fori_loop(skipped + 1, count, step, 0)


def kernel(dims, factor, names, feat, adj1, pre_any, adj2, w2_any, og_any, out1, out2, outb, *scratch):
    v = types.SimpleNamespace(**dict(zip(names, scratch)))
    Y, X, Z, G, C = dims
    NP, ZZ = Y * X, Z * G
    y, x, z, g, c = (lax.axis_index(a) for a in AXES)
    me = y * X + x
    zabs = g * Z + z
    relations = v.words1.shape[0] // Z
    half = (relations + 1) // C
    cw = feat.shape[2]
    seeds, h = v.og.shape
    dst = v.pre.shape[0]
    hc = h // NP
    base = me * Z
    partner = (y, x, z, g, 1 - c)
    across = (y, x, z, 1 - g, c)

    def send_sem(phase, q=0):
        return v.ss.at[phase * half + q]

    def recv_sem(phase, q=0):
        return v.rs.at[phase * half + q]

    def over_plane(body, sign=1):
        def step(t):
            dy = lax.rem(Y // 2 + lax.div(t, X), Y)
            dx = lax.rem(X // 2 + lax.rem(t, X), X)
            yy = lax.rem(y + sign * dy + Y, Y)
            xx = lax.rem(x + sign * dx + X, X)
            body(dy * X + dx, yy * X + xx, (yy, xx, z, g, c))

        skip_loop(NP, (Y - Y // 2) * X + X - X // 2 if X > 1 else Y - Y // 2, step)

    def over_column(body):
        def step(t):
            zz = lax.rem(zabs + ZZ // 2 + t, ZZ)
            body((y, x, lax.rem(zz, Z), lax.div(zz, Z), c))

        skip_loop(ZZ, ZZ - ZZ // 2, step)

    def minibatch(i):
        return lax.rem(z + i, 2) + 2 * lax.rem(lax.div(z, 2) + i // 2 if isinstance(i, int) else lax.div(z, 2) + lax.div(i, 2), 2)

    barrier = pltpu.get_barrier_semaphore()

    def greet(device):
        pl.semaphore_signal(barrier, inc=1, device_id=device, device_id_type=MESH)

    over_plane(lambda slot, other, device: greet(device))
    over_column(greet)
    greet(partner)

    loads = [
        local(adj2.at[0, 0], v.words2, v.loc.at[0]),
        local(pre_any.at[0, 0], v.pre, v.loc.at[1]),
        local(og_any.at[0, 0], v.og, v.loc.at[2]),
        local(w2_any, v.w2, v.loc.at[3]),
        local(feat.at[0], v.xv, v.loc.at[4]),
    ]
    for q in range(Z):
        loads.append(
            local(adj1.at[0, base + q], v.words1.at[pl.ds(q * relations, relations)], v.loc.at[5 + q])
        )
    for load in loads:
        load.start()
    v.rx[:, pl.ds(0, TOP), :] = jnp.ones((Z, TOP, v.rx.shape[2]), BF16)
    loads[0].wait()
    for r in range(relations):
        spread_bits(v.words2, r, v.dense2, seeds, h)

    for load in loads[1:4]:
        load.wait()
    hidden = jnp.maximum(v.pre[...], 0)
    scaled = v.og[...].astype(F32) * factor
    low = scaled.astype(BF16)
    ones = jnp.ones((h, h), BF16)
    v.wg[0] = mm(hidden[:seeds], low, TN)
    v.total[...] = jnp.zeros_like(v.total)
    v.total[pl.ds(0, seeds), :] = mm(low, v.w2[0], NT)
    for r in range(relations):
        dense = v.dense2[r]
        inverse = 1.0 / jnp.maximum(mm(dense, ones, NN), 1.0)
        mixed = (mm(dense, hidden, NN) * inverse).astype(BF16)
        v.wg[r + 1] = mm(mixed, low, TN)
        backed = (mm(low, v.w2[r + 1], NT) * inverse).astype(BF16)
        v.total[...] += mm(dense, backed, TN)
    grad = jnp.where(v.pre[...] > 0, v.total[...], 0.0).astype(BF16)
    v.hgown[...] = grad
    local(v.hgown, v.hgbuf.at[z], v.hr.at[0]).start()
    row = lax.broadcasted_iota(jnp.int32, (BIAS, h), 0)
    bias_one = jnp.sum(grad.astype(F32), axis=0, keepdims=True)
    bias_two = jnp.sum(scaled, axis=0, keepdims=True)
    first = c == 0
    bias_keep = jnp.where(row == 0, jnp.where(first, bias_one, bias_two), 0.0)
    bias_give = jnp.where(row == 0, jnp.where(first, bias_two, bias_one), 0.0)
    for q in range(half):
        v.cxs2[pl.ds(q * h, h), :] = v.wg[(1 - c) * half + q].astype(BF16)
    v.cxs2[pl.ds(half * h, BIAS), :] = bias_give.astype(BF16)
    loads[4].wait()

    pl.semaphore_wait(barrier, NP + ZZ - 1)

    swap2 = remote(v.cxs2, v.cxr2, send_sem(SWAP2), recv_sem(SWAP2), partner)
    swap2.start()

    def give_grad(k):
        return remote(v.hgown, v.hgbuf.at[z], v.hs.at[k], v.hr.at[k], (y, x, minibatch(k), g, c))

    for k in range(1, Z):
        give_grad(k).start()

    for i in range(Z):
        m = minibatch(i)
        local(v.xv.at[base + m], v.rx.at[m, pl.ds(TOP, cw), :], v.own.at[i]).start()
        over_plane(
            lambda slot, other, device: remote(
                v.xv.at[other * Z + m],
                v.rx.at[m, pl.ds(pl.multiple_of(TOP + slot * cw, cw), cw), :],
                v.xs.at[i],
                v.xr.at[i],
                device,
            ).start()
        )

    for load in loads[5:]:
        load.wait()

    def spread_one(t, carry):
        spread_scaled(v.words1, t, v.dense1, 16 * v.words1.shape[1], v.words1.shape[2])
        return carry

    lax.fori_loop(0, Z * relations, spread_one, 0)

    swap2.wait_recv()
    bias = (bias_keep + v.cxr2[pl.ds(half * h, BIAS), :].astype(F32)).astype(BF16)
    v.s2_0[:, pl.ds(hc, BIAS), :] = jnp.broadcast_to(bias[None], (NP, BIAS, h))
    s2 = [getattr(v, f"s2_{q}") for q in range(half)]
    r2 = [getattr(v, f"r2_{q}") for q in range(half)]
    zb = [getattr(v, f"zb_{q}") for q in range(half)]
    ag = [getattr(v, f"ag_{q}") for q in range(half)]
    agp = [getattr(v, f"agp_{q}") for q in range(half)]
    for q in range(half):
        both = v.wg[c * half + q] + v.cxr2[pl.ds(q * h, h), :].astype(F32)
        s2[q][:, pl.ds(0, hc), :] = both.astype(BF16).reshape(NP, hc, h)
        over_plane(
            lambda slot, other, device: remote(
                s2[q].at[other], r2[q].at[slot], send_sem(RS2, q), recv_sem(RS2, q), device
            ).start()
        )

    v.acc[...] = jnp.zeros_like(v.acc)
    least = lax.shift_left(1, lax.rem(lax.broadcasted_iota(jnp.int32, (1, dst), 1), 16)).astype(F32)

    def one_minibatch(i, carry):
        m = minibatch(i)
        local(v.xv.at[base + m], v.rx.at[m, pl.ds(TOP, cw), :], v.own.at[i]).wait()
        arrived = v.rx.at[m, pl.ds(TOP + cw, (NP - 1) * cw), :]
        local(arrived, arrived, v.xr.at[i]).wait()
        local(v.hgown, v.hgbuf.at[m], v.hr.at[i]).wait()
        grad_m = v.hgbuf[m]
        v.acc[0] += mm(v.rx[m, pl.ds(TOP, NP * cw), pl.ds(0, dst)], grad_m, NN)
        for r in range(relations):
            product = mm(v.rx[m], v.dense1[m * relations + r], NT)
            weight = 1.0 / jnp.maximum(product[:1], least)
            v.gathered[r] = (product[TOP:] * weight).astype(BF16)
        for r in range(relations):
            v.acc[r + 1] += mm(v.gathered[r], grad_m, NN)
        return carry

    lax.fori_loop(0, Z, one_minibatch, 0)

    def swap1(q):
        return remote(v.cxs1.at[q], v.cxr1.at[q], send_sem(SWAP1, q), recv_sem(SWAP1, q), partner)

    for q in range(half):
        v.cxs1[q] = v.acc[(1 - c) * half + q].astype(BF16)
        swap1(q).start()

    def second_sum(q):
        arrived = r2[q].at[pl.ds(1, NP - 1)]
        local(arrived, arrived, recv_sem(RS2, q)).wait()
        summed = s2[q][me].astype(F32)
        for k in range(1, NP):
            summed += r2[q][k].astype(F32)
        zb[q][zabs] = summed.astype(BF16)
        over_column(
            lambda device: remote(
                zb[q].at[zabs], zb[q].at[zabs], send_sem(COL, q), recv_sem(COL, q), device
            ).start()
        )

    def column_sum(q):
        arrived = zb[q].at[pl.ds(0, ZZ - 1)]
        local(arrived, arrived, recv_sem(COL, q)).wait()
        summed = zb[q][0].astype(F32)
        for k in range(1, ZZ):
            summed += zb[q][k].astype(F32)
        ag[q][me] = summed.astype(BF16)
        over_plane(
            lambda slot, other, device: remote(
                ag[q].at[me], ag[q].at[me], send_sem(AG, q), recv_sem(AG, q), device
            ).start()
        )

    second_sum(0)

    for q in range(half):
        swap1(q).wait_recv()
        both = v.acc[c * half + q] + v.cxr1[q].astype(F32)
        v.s1[q] = both.astype(BF16).reshape(NP, cw, h)
        over_plane(
            lambda slot, other, device: remote(
                v.s1.at[q, slot], v.r1.at[q, slot], send_sem(RS1, q), recv_sem(RS1, q), device
            ).start(),
            -1,
        )

    for q in range(1, half):
        second_sum(q)

    for q in range(half):
        column_sum(q)

    for q in range(half):
        arrived = v.r1.at[q, pl.ds(1, NP - 1)]
        local(arrived, arrived, recv_sem(RS1, q)).wait()
        summed = v.s1[q, 0].astype(F32)
        for k in range(1, NP):
            summed += v.r1[q, k].astype(F32)
        v.zhs[q] = summed.astype(BF16)
    cross = remote(v.zhs, v.zhr, send_sem(CROSS), recv_sem(CROSS), across)
    cross.start()

    def swap3(q):
        return remote(ag[q], agp[q], send_sem(SWAP3, q), recv_sem(SWAP3, q), partner)

    stores = []

    def store(src, dst_ref):
        stores.append(local(src, dst_ref, v.st.at[len(stores)]))
        stores[-1].start()

    for q in range(half):
        arrived = ag[q].at[pl.ds(0, NP - 1)]
        local(arrived, arrived, recv_sem(AG, q)).wait()
        swap3(q).start()
        store(ag[q].at[:, pl.ds(0, hc), :], out2.at[c * half + q])

    cross.wait_recv()
    v.d1s[...] = v.zhs[...].astype(F32) + v.zhr[...].astype(F32)
    swap4 = remote(v.d1s, v.d1r, send_sem(SWAP4), recv_sem(SWAP4), partner)
    swap4.start()
    store(v.d1s, out1.at[pl.ds(c * half, half)])

    for q in range(half):
        swap3(q).wait_recv()
        store(agp[q].at[:, pl.ds(0, hc), :], out2.at[(1 - c) * half + q])
        if q == 0:
            kept = ag[0][0, pl.ds(hc, BIAS), :].astype(F32)[:1]
            given = agp[0][0, pl.ds(hc, BIAS), :].astype(F32)[:1]
            v.bias[...] = jnp.where(row == c, kept, given)
            store(v.bias, outb)

    swap4.wait_recv()
    store(v.d1r, out1.at[pl.ds((1 - c) * half, half)])

    for i in range(Z):
        sent = v.xv.at[pl.ds(0, NP - 1)]
        local(sent, sent, v.xs.at[i]).wait()
    for k in range(1, Z):
        give_grad(k).wait_send()
    for swap in (swap2, cross, swap4):
        swap.wait_send()
    for q in range(half):
        swap1(q).wait_send()
        swap3(q).wait_send()
        for phase, ref in (
            (RS2, r2[q].at[pl.ds(1, NP - 1)]),
            (COL, zb[q].at[pl.ds(0, ZZ - 1)]),
            (AG, ag[q].at[pl.ds(0, NP - 1)]),
            (RS1, v.r1.at[q, pl.ds(1, NP - 1)]),
        ):
            local(ref, ref, send_sem(phase, q)).wait()
    for copy in stores:
        copy.wait()


def on_device(dims, features, adjacency_one, pre_hidden, adjacency_two, weight_two, out_grad):
    Y, X, Z, G, C = dims
    NP, ZZ = Y * X, Z * G
    blocks, cw, nb = features.shape[1:]
    relations, word_rows = adjacency_one.shape[2:4]
    dst, h = pre_hidden.shape[2:]
    seeds = out_grad.shape[2]
    half = (relations + 1) // C
    hc = h // NP
    factor = float(seeds * NP * ZZ * C) ** (-0.5)
    vmem = pltpu.VMEM
    any_spec = pl.BlockSpec(memory_space=pl.ANY)
    dma = pltpu.SemaphoreType.DMA
    shapes = dict(
        pre=vmem((dst, h), BF16),
        words2=vmem(adjacency_two.shape[2:], jnp.int32),
        w2=vmem(weight_two.shape, BF16),
        og=vmem((seeds, h), BF16),
        xv=vmem((blocks, cw, nb), BF16),
        words1=vmem((Z * relations, word_rows, nb), jnp.int32),
        dense2=vmem((relations, seeds, dst), BF16),
        dense1=vmem((Z * relations, dst, nb), BF16),
        rx=vmem((Z, TOP + NP * cw, nb), BF16),
        hgown=vmem((dst, h), BF16),
        hgbuf=vmem((Z, dst, h), BF16),
        gathered=vmem((relations, NP * cw, dst), BF16),
        total=vmem((dst, h), F32),
        acc=vmem((relations + 1, NP * cw, h), F32),
        wg=vmem((relations + 1, h, h), F32),
        cxs2=vmem((half * h + BIAS, h), BF16),
        cxr2=vmem((half * h + BIAS, h), BF16),
        cxs1=vmem((half, NP * cw, h), BF16),
        cxr1=vmem((half, NP * cw, h), BF16),
        s1=vmem((half, NP, cw, h), BF16),
        r1=vmem((half, NP, cw, h), BF16),
        zhs=vmem((half, cw, h), BF16),
        zhr=vmem((half, cw, h), BF16),
        d1s=vmem((half, cw, h), F32),
        d1r=vmem((half, cw, h), F32),
        bias=vmem((BIAS, h), F32),
        loc=dma((5 + Z,)),
        own=dma((Z,)),
        xs=dma((Z,)),
        xr=dma((Z,)),
        hs=dma((Z,)),
        hr=dma((Z,)),
        ss=dma((9 * half,)),
        rs=dma((9 * half,)),
        st=dma((2 * half + 3,)),
    )
    for q in range(half):
        rows = hc + (BIAS if q == 0 else 0)
        for name in ("s2", "r2", "ag", "agp"):
            shapes[f"{name}_{q}"] = vmem((NP, rows, h), BF16)
        shapes[f"zb_{q}"] = vmem((ZZ, rows, h), BF16)
    out1, out2, outb = pl.pallas_call(
        functools.partial(kernel, dims, factor, tuple(shapes)),
        name="graph_grads",
        out_shape=(
            jax.ShapeDtypeStruct((relations + 1, cw, h), F32),
            jax.ShapeDtypeStruct((relations + 1, NP, hc, h), BF16),
            jax.ShapeDtypeStruct((BIAS, h), F32),
        ),
        in_specs=[any_spec] * 6,
        out_specs=(any_spec,) * 3,
        scratch_shapes=list(shapes.values()),
        compiler_params=pltpu.CompilerParams(
            collective_id=0, has_side_effects=True, vmem_limit_bytes=66000000
        ),
    )(features, adjacency_one, pre_hidden, adjacency_two, weight_two, out_grad)
    return out1, outb[0], out2.reshape(relations + 1, h, h).astype(F32), outb[1]


def build(devices, dims):
    torus = Mesh(devices.reshape(dims), AXES)
    placed = (
        P(REP, None, FEAT, None),
        P(REP, None, None, None, None),
        P(REP, FEAT, None, None),
        P(REP, FEAT, None, None, None),
        P(),
        P(REP, FEAT, None, None),
    )
    return jax.shard_map(
        functools.partial(on_device, dims),
        mesh=torus,
        in_specs=placed,
        out_specs=(P(None, FEAT, None), P(), P(), P()),
        check_vma=False,
    )


def solution(mesh):
    dims = (4, 4, mesh.shape["feat"] // 16, mesh.shape["rep"] // 2, 2)
    return build(mesh.devices, dims)
```

time: 496 us -> 49.5 us (0.10)
  other arithmetic: 149 us -> 2.42 us
  waiting for transfers between devices: 120 us -> 0 us
  blocking collectives: 93.4 us -> 0 us
  matrix products: 76.7 us -> 0 us
  Pallas kernels: 0 us -> 44.2 us
  local copies, waits for them, and re-layouts: 32.2 us -> 1.99 us
  between operations: 15.6 us -> 0.65 us
  starting transfers between devices: 7.95 us -> 0 us
    all_gather x2 -> x0, waiting for transfers between devices: 120 us -> none  [all_blocks(): tiles = lax.all_gather(tiles, axes[k])]
    reduce_sum x10 -> x0, other arithmetic: 87.6 us -> none  [the longest x8 86.9 us: unpack(): degree = jnp.sum(dense, axis=-1).astype(jnp.float32)]
    dot_general x20 -> x0, matrix products: 76.7 us -> none  [the longest x8 59.3 us: panel_terms(): jnp.einsum('brdc,bdh->rch', gathered, grad_block, preferred_element_type=...]
    psum x1 -> x0, blocking collectives: 76.6 us -> none  [on_device(): lax.psum((weight_grad, bias_one, bias_two), FEAT_REP)]
    convert_element_type x10 -> x1, other arithmetic: 58.2 us -> 2.42 us  [on_device(): out2.reshape(relations + 1, h, h).astype(F32)]
    pallas_call x0 -> x1, Pallas kernels: none -> 44.2 us  [on_device(): pl.pallas_call(functools.partial(kernel, dims, factor, tuple(shapes)), na...]
    all_gather x1 -> x0, blocking collectives: 16.8 us -> none  [all_blocks(): tiles = lax.all_gather(tiles, axes[k])]
    shift_right_arithmetic x26 -> x0, local copies, waits for them, and re-layouts: 12.2 us -> none  [unpack(): jnp.right_shift(packed[..., None, :], shifts[:, None])]
  transfers between devices with their start and end apart: 4 -> 0, of which waited for: 2 -> 0; matrix products, arithmetic and copies ran while one was open for 50% -> 0% of each run, Pallas kernels for 0% -> 0%
where the time goes in v2:
time: 49.5 us; the launch traced here: 49.3 us
  Pallas kernels  44.2 us (89%)
  other arithmetic  2.42 us (5%)
  local copies, waits for them, and re-layouts  1.99 us (4%)
  between operations  0.65 us (1%)
    pallas_call x1, Pallas kernels, on_device(): pl.pallas_call(functools.partial(kernel, dims, factor, tuple(shapes)), na...  44.2 us
    convert_element_type x1, other arithmetic, on_device(): out2.reshape(relations + 1, h, h).astype(F32)  2.42 us
    slice x1, local copies, waits for them, and re-layouts, on_device(): outb[1]  1.34 us

profile of v2, /device:TPU:1, one launch (start us, length us, event | category | flops | bytes accessed | tf_op | source)
XLA Modules:
  0.0 49.3 jit_solution(783283284960451503)
XLA Ops:
  0.6 44.2 %graph_grads.1 = (f32[6,16,256]{2,1,0:T(8,128)}, bf16[6,16,16,256]{3,2,1,0:T(8,128)(2,1)}, f32[8,256]{1,0:T(8,128)}) custom-call(bf16[1,64,16,512]{3,2,1,0:T(8,128)(2,1)} %feat.1, s32[1,64,5,16,512]{4,3,2,1,0:T(8,128)} %adj1.1, bf16[1,1,256,256]{3,2,1,0:T(8,128)(2,1)} %pre_any.1, s32[1,1,5,8,256]{4,3,2,1,0:T(8,128)} %adj2.1, bf16[6,256,256]{2,1,0:T(8,128)(2,1)} %w2_any.1, ...), custom_call_target="tpu_custom_call" | custom-call | tf_op jit(solution)/shard_map/graph_grads/pallas_call | solution.py:407
  44.9 0.0 copy-start
  44.9 1.3 %fusion = (f32[1,256]{1,0:T(1,128)}, f32[1,256]{1,0:T(1,128)}) fusion(f32[8,256]{1,0:T(8,128)} %get-tuple-element.8), kind=kLoop, calls=%fused_computation.1 | loop fusion | bytes 4096 | tf_op jit(solution)/shard_map/slice | solution.py:422
  46.2 2.4 %bitcast_convert_fusion = f32[6,256,256]{2,1,0:T(8,128)} fusion(bf16[6,16,16,256]{3,2,1,0:T(8,128)(2,1)} %get-tuple-element.9), kind=kLoop, calls=%fused_computation | loop fusion | flops 393216 | bytes 2359296 | tf_op jit(solution)/shard_map/convert_element_type | solution.py:422
  48.6 0.0 copy-done
  48.6 0.6 %copy.11 = f32[6,16,256]{2,1,0:T(8,128)} copy(f32[6,16,256]{2,1,0:T(8,128)S(1)} %copy-done) | data formatting | bytes 196608
Async XLA Ops:
  44.9 3.8 %copy-start = (f32[6,16,256]{2,1,0:T(8,128)S(1)}, f32[6,16,256]{2,1,0:T(8,128)}, u32[]{:S(2)}) copy-start(f32[6,16,256]{2,1,0:T(8,128)} %get-tuple-element.16) | copy-start | bytes 294916

commit v3 on v2

--- a/solution.py
+++ b/solution.py
@@ -18,9 +18,12 @@
 NN = (((1,), (0,)), ((), ()))
 NT = (((1,), (1,)), ((), ()))
 TN = (((0,), (0,)), ((), ()))
+WIDEN_LIMIT = 66000000
+MAIN_LIMIT = 66000000
 TOP = 16
-BIAS = 8
-SWAP2, RS2, COL, AG, SWAP3, SWAP1, RS1, CROSS, SWAP4 = range(9)
+PARTS = 1
+PHASES = 13
+SWAP2, RS2, COL, AG, SWAP3, SWAP1, RS1, CROSS, SWAP4, BSWAP, BPLANE, BCOL, BLAST = range(PHASES)
 
 
 def mm(a, b, dims):
@@ -75,25 +78,27 @@
     seeds, h = v.og.shape
     dst = v.pre.shape[0]
     hc = h // NP
+    chunks = [(q, p) for q in range(half) for p in range(PARTS)]
+    pc = hc // PARTS
     base = me * Z
     partner = (y, x, z, g, 1 - c)
     across = (y, x, z, 1 - g, c)
 
     def send_sem(phase, q=0):
-        return v.ss.at[phase * half + q]
+        return v.ss.at[phase * len(chunks) + q]
 
     def recv_sem(phase, q=0):
-        return v.rs.at[phase * half + q]
+        return v.rs.at[phase * len(chunks) + q]
+
+    rows_of = [lax.rem(y + d, Y) for d in range(Y)]
+    cols_of = [lax.rem(x + d, X) for d in range(X)]
+    pairs = [(dy, dx) for dy in range(Y) for dx in range(X) if dy or dx]
+    pairs.sort(key=lambda p: -min(p[0], Y - p[0]) - min(p[1], X - p[1]))
 
     def over_plane(body, sign=1):
-        def step(t):
-            dy = lax.rem(Y // 2 + lax.div(t, X), Y)
-            dx = lax.rem(X // 2 + lax.rem(t, X), X)
-            yy = lax.rem(y + sign * dy + Y, Y)
-            xx = lax.rem(x + sign * dx + X, X)
+        for dy, dx in pairs:
+            yy, xx = rows_of[(sign * dy) % Y], cols_of[(sign * dx) % X]
             body(dy * X + dx, yy * X + xx, (yy, xx, z, g, c))
-
-        skip_loop(NP, (Y - Y // 2) * X + X - X // 2 if X > 1 else Y - Y // 2, step)
 
     def over_column(body):
         def step(t):
@@ -134,38 +139,21 @@
 
     for load in loads[1:4]:
         load.wait()
-    hidden = jnp.maximum(v.pre[...], 0)
     scaled = v.og[...].astype(F32) * factor
     low = scaled.astype(BF16)
     ones = jnp.ones((h, h), BF16)
-    v.wg[0] = mm(hidden[:seeds], low, TN)
     v.total[...] = jnp.zeros_like(v.total)
     v.total[pl.ds(0, seeds), :] = mm(low, v.w2[0], NT)
     for r in range(relations):
-        dense = v.dense2[r]
-        inverse = 1.0 / jnp.maximum(mm(dense, ones, NN), 1.0)
-        mixed = (mm(dense, hidden, NN) * inverse).astype(BF16)
-        v.wg[r + 1] = mm(mixed, low, TN)
+        inverse = 1.0 / jnp.maximum(mm(v.dense2[r], ones, NN), 1.0)
+        v.weight2[r] = inverse
         backed = (mm(low, v.w2[r + 1], NT) * inverse).astype(BF16)
-        v.total[...] += mm(dense, backed, TN)
-    grad = jnp.where(v.pre[...] > 0, v.total[...], 0.0).astype(BF16)
-    v.hgown[...] = grad
+        v.total[...] += mm(v.dense2[r], backed, TN)
+    v.hgown[...] = jnp.where(v.pre[...] > 0, v.total[...], 0.0).astype(BF16)
     local(v.hgown, v.hgbuf.at[z], v.hr.at[0]).start()
-    row = lax.broadcasted_iota(jnp.int32, (BIAS, h), 0)
-    bias_one = jnp.sum(grad.astype(F32), axis=0, keepdims=True)
-    bias_two = jnp.sum(scaled, axis=0, keepdims=True)
-    first = c == 0
-    bias_keep = jnp.where(row == 0, jnp.where(first, bias_one, bias_two), 0.0)
-    bias_give = jnp.where(row == 0, jnp.where(first, bias_two, bias_one), 0.0)
-    for q in range(half):
-        v.cxs2[pl.ds(q * h, h), :] = v.wg[(1 - c) * half + q].astype(BF16)
-    v.cxs2[pl.ds(half * h, BIAS), :] = bias_give.astype(BF16)
     loads[4].wait()
 
     pl.semaphore_wait(barrier, NP + ZZ - 1)
-
-    swap2 = remote(v.cxs2, v.cxr2, send_sem(SWAP2), recv_sem(SWAP2), partner)
-    swap2.start()
 
     def give_grad(k):
         return remote(v.hgown, v.hgbuf.at[z], v.hs.at[k], v.hr.at[k], (y, x, minibatch(k), g, c))
@@ -173,18 +161,40 @@
     for k in range(1, Z):
         give_grad(k).start()
 
-    for i in range(Z):
+    def send_features(i, carry):
         m = minibatch(i)
         local(v.xv.at[base + m], v.rx.at[m, pl.ds(TOP, cw), :], v.own.at[i]).start()
         over_plane(
             lambda slot, other, device: remote(
                 v.xv.at[other * Z + m],
-                v.rx.at[m, pl.ds(pl.multiple_of(TOP + slot * cw, cw), cw), :],
+                v.rx.at[m, pl.ds(TOP + slot * cw, cw), :],
                 v.xs.at[i],
                 v.xr.at[i],
                 device,
             ).start()
         )
+        return carry
+
+    lax.fori_loop(0, Z, send_features, 0)
+
+    hidden = jnp.maximum(v.pre[...], 0)
+    scaled = v.og[...].astype(F32) * factor
+    low = scaled.astype(BF16)
+    v.wg[0] = mm(hidden[:seeds], low, TN)
+    for r in range(relations):
+        mixed = (mm(v.dense2[r], hidden, NN) * v.weight2[r]).astype(BF16)
+        v.wg[r + 1] = mm(mixed, low, TN)
+    bias_one = jnp.sum(v.hgown[...].astype(F32), axis=0, keepdims=True)
+    bias_two = jnp.sum(scaled, axis=0, keepdims=True)
+    first = c == 0
+    bias_keep = jnp.where(first, bias_one, bias_two)
+    v.bs[...] = jnp.where(first, bias_two, bias_one)
+    for q in range(half):
+        v.cxs2[pl.ds(q * h, h), :] = v.wg[(1 - c) * half + q].astype(BF16)
+    swap2 = remote(v.cxs2, v.cxr2, send_sem(SWAP2), recv_sem(SWAP2), partner)
+    swap2.start()
+    bias_swap = remote(v.bs, v.br, send_sem(BSWAP), recv_sem(BSWAP), partner)
+    bias_swap.start()
 
     for load in loads[5:]:
         load.wait()
@@ -195,20 +205,25 @@
 
     lax.fori_loop(0, Z * relations, spread_one, 0)
 
+    bias_swap.wait_recv()
+    v.bplane[me] = bias_keep + v.br[...]
+    over_plane(
+        lambda slot, other, device: remote(
+            v.bplane.at[me], v.bplane.at[me], send_sem(BPLANE), recv_sem(BPLANE), device
+        ).start()
+    )
+    s2 = [getattr(v, f"s2_{n}") for n in range(len(chunks))]
+    r2 = [getattr(v, f"r2_{n}") for n in range(len(chunks))]
+    zb = [getattr(v, f"zb_{n}") for n in range(len(chunks))]
+    ag = [getattr(v, f"ag_{n}") for n in range(len(chunks))]
     swap2.wait_recv()
-    bias = (bias_keep + v.cxr2[pl.ds(half * h, BIAS), :].astype(F32)).astype(BF16)
-    v.s2_0[:, pl.ds(hc, BIAS), :] = jnp.broadcast_to(bias[None], (NP, BIAS, h))
-    s2 = [getattr(v, f"s2_{q}") for q in range(half)]
-    r2 = [getattr(v, f"r2_{q}") for q in range(half)]
-    zb = [getattr(v, f"zb_{q}") for q in range(half)]
-    ag = [getattr(v, f"ag_{q}") for q in range(half)]
-    agp = [getattr(v, f"agp_{q}") for q in range(half)]
-    for q in range(half):
-        both = v.wg[c * half + q] + v.cxr2[pl.ds(q * h, h), :].astype(F32)
-        s2[q][:, pl.ds(0, hc), :] = both.astype(BF16).reshape(NP, hc, h)
+    for n, (q, p) in enumerate(chunks):
+        if p == 0:
+            both = (v.wg[c * half + q] + v.cxr2[pl.ds(q * h, h), :].astype(F32)).astype(BF16).reshape(NP, hc, h)
+        s2[n][...] = both[:, p * pc : (p + 1) * pc]
         over_plane(
             lambda slot, other, device: remote(
-                s2[q].at[other], r2[q].at[slot], send_sem(RS2, q), recv_sem(RS2, q), device
+                s2[n].at[other], r2[n].at[slot], send_sem(RS2, n), recv_sem(RS2, n), device
             ).start()
         )
 
@@ -266,37 +281,51 @@
             ).start()
         )
 
-    second_sum(0)
-
     for q in range(half):
         swap1(q).wait_recv()
         both = v.acc[c * half + q] + v.cxr1[q].astype(F32)
-        v.s1[q] = both.astype(BF16).reshape(NP, cw, h)
-        over_plane(
-            lambda slot, other, device: remote(
-                v.s1.at[q, slot], v.r1.at[q, slot], send_sem(RS1, q), recv_sem(RS1, q), device
-            ).start(),
-            -1,
-        )
-
-    for q in range(1, half):
-        second_sum(q)
-
-    for q in range(half):
-        column_sum(q)
-
-    for q in range(half):
-        arrived = v.r1.at[q, pl.ds(1, NP - 1)]
-        local(arrived, arrived, recv_sem(RS1, q)).wait()
-        summed = v.s1[q, 0].astype(F32)
-        for k in range(1, NP):
-            summed += v.r1[q, k].astype(F32)
-        v.zhs[q] = summed.astype(BF16)
+        v.s1[:, pl.ds(q * cw, cw), :] = both.astype(BF16).reshape(NP, cw, h)
+    over_plane(
+        lambda slot, other, device: remote(
+            v.s1.at[slot], v.r1.at[slot], send_sem(RS1), recv_sem(RS1), device
+        ).start(),
+        -1,
+    )
+
+    for n in range(len(chunks)):
+        second_sum(n)
+    bias_in = v.bplane.at[pl.ds(0, NP - 1)]
+    local(bias_in, bias_in, recv_sem(BPLANE)).wait()
+    v.bcol[zabs] = jnp.sum(v.bplane[...], axis=0)
+    over_column(
+        lambda device: remote(
+            v.bcol.at[zabs], v.bcol.at[zabs], send_sem(BCOL), recv_sem(BCOL), device
+        ).start()
+    )
+
+    for n in range(len(chunks)):
+        column_sum(n)
+
+    first_in = v.r1.at[pl.ds(1, NP - 1)]
+    local(first_in, first_in, recv_sem(RS1)).wait()
+    summed = v.s1[0].astype(F32)
+    for k in range(1, NP):
+        summed += v.r1[k].astype(F32)
+    v.zhs[...] = summed.astype(BF16).reshape(half, cw, h)
     cross = remote(v.zhs, v.zhr, send_sem(CROSS), recv_sem(CROSS), across)
     cross.start()
-
-    def swap3(q):
-        return remote(ag[q], agp[q], send_sem(SWAP3, q), recv_sem(SWAP3, q), partner)
+    bias_col = v.bcol.at[pl.ds(0, ZZ - 1)]
+    local(bias_col, bias_col, recv_sem(BCOL)).wait()
+    v.bmine[...] = jnp.sum(v.bcol[...], axis=0)
+    bias_last = remote(v.bmine, v.btheirs, send_sem(BLAST), recv_sem(BLAST), partner)
+    bias_last.start()
+
+    def panel_part(n):
+        q, p = chunks[n]
+        return out2.at[c * half + q, :, pl.ds(p * pc, pc), :]
+
+    def swap3(n):
+        return remote(ag[n], panel_part(n), send_sem(SWAP3, n), recv_sem(SWAP3, n), partner)
 
     stores = []
 
@@ -304,49 +333,71 @@
         stores.append(local(src, dst_ref, v.st.at[len(stores)]))
         stores[-1].start()
 
-    for q in range(half):
-        arrived = ag[q].at[pl.ds(0, NP - 1)]
-        local(arrived, arrived, recv_sem(AG, q)).wait()
-        swap3(q).start()
-        store(ag[q].at[:, pl.ds(0, hc), :], out2.at[c * half + q])
+    for n in range(len(chunks)):
+        arrived = ag[n].at[pl.ds(0, NP - 1)]
+        local(arrived, arrived, recv_sem(AG, n)).wait()
+        swap3(n).start()
+        store(ag[n], panel_part(n))
 
     cross.wait_recv()
     v.d1s[...] = v.zhs[...].astype(F32) + v.zhr[...].astype(F32)
-    swap4 = remote(v.d1s, v.d1r, send_sem(SWAP4), recv_sem(SWAP4), partner)
+    swap4 = remote(v.d1s, out1.at[pl.ds(c * half, half)], send_sem(SWAP4), recv_sem(SWAP4), partner)
     swap4.start()
     store(v.d1s, out1.at[pl.ds(c * half, half)])
 
-    for q in range(half):
-        swap3(q).wait_recv()
-        store(agp[q].at[:, pl.ds(0, hc), :], out2.at[(1 - c) * half + q])
-        if q == 0:
-            kept = ag[0][0, pl.ds(hc, BIAS), :].astype(F32)[:1]
-            given = agp[0][0, pl.ds(hc, BIAS), :].astype(F32)[:1]
-            v.bias[...] = jnp.where(row == c, kept, given)
-            store(v.bias, outb)
+    bias_last.wait_recv()
+    mine, theirs = v.bmine[...], v.btheirs[...]
+    row = lax.broadcasted_iota(jnp.int32, (8, h), 0)
+    v.bias[...] = jnp.where(row == c, mine, theirs)
+    store(v.bias, outb)
+
+    for n in range(len(chunks)):
+        swap3(n).wait_recv()
 
     swap4.wait_recv()
-    store(v.d1r, out1.at[pl.ds((1 - c) * half, half)])
 
     for i in range(Z):
         sent = v.xv.at[pl.ds(0, NP - 1)]
         local(sent, sent, v.xs.at[i]).wait()
     for k in range(1, Z):
         give_grad(k).wait_send()
-    for swap in (swap2, cross, swap4):
+    for swap in (swap2, cross, swap4, bias_swap, bias_last):
         swap.wait_send()
     for q in range(half):
         swap1(q).wait_send()
-        swap3(q).wait_send()
+    for n in range(len(chunks)):
+        swap3(n).wait_send()
         for phase, ref in (
-            (RS2, r2[q].at[pl.ds(1, NP - 1)]),
-            (COL, zb[q].at[pl.ds(0, ZZ - 1)]),
-            (AG, ag[q].at[pl.ds(0, NP - 1)]),
-            (RS1, v.r1.at[q, pl.ds(1, NP - 1)]),
+            (RS2, r2[n].at[pl.ds(1, NP - 1)]),
+            (COL, zb[n].at[pl.ds(0, ZZ - 1)]),
+            (AG, ag[n].at[pl.ds(0, NP - 1)]),
         ):
-            local(ref, ref, send_sem(phase, q)).wait()
+            local(ref, ref, send_sem(phase, n)).wait()
+    local(bias_in, bias_in, send_sem(BPLANE)).wait()
+    local(bias_col, bias_col, send_sem(BCOL)).wait()
+    local(first_in, first_in, send_sem(RS1)).wait()
     for copy in stores:
         copy.wait()
+
+
+def widen(first_in, second_in, bias_in, first, second, bias_one, bias_two, one, low, wide, bias, come, go):
+    panels = low.shape[0]
+    gets = [local(second_in.at[r], low.at[r], come.at[r]) for r in range(panels)]
+    gets += [local(first_in, one, come.at[panels]), local(bias_in, bias, come.at[panels + 1])]
+    puts = [local(wide.at[r], second.at[r], go.at[r]) for r in range(panels)] + [local(one, first, go.at[panels])]
+    for get in gets:
+        get.start()
+    for r in range(panels):
+        gets[r].wait()
+        wide[r] = low[r].astype(F32)
+        puts[r].start()
+    gets[panels].wait()
+    puts[panels].start()
+    gets[panels + 1].wait()
+    bias_one[...] = bias[:1]
+    bias_two[...] = bias[1:2]
+    for put in puts:
+        put.wait()
 
 
 def on_device(dims, features, adjacency_one, pre_hidden, adjacency_two, weight_two, out_grad):
@@ -376,50 +427,78 @@
         hgbuf=vmem((Z, dst, h), BF16),
         gathered=vmem((relations, NP * cw, dst), BF16),
         total=vmem((dst, h), F32),
+        weight2=vmem((relations, seeds, dst), F32),
         acc=vmem((relations + 1, NP * cw, h), F32),
         wg=vmem((relations + 1, h, h), F32),
-        cxs2=vmem((half * h + BIAS, h), BF16),
-        cxr2=vmem((half * h + BIAS, h), BF16),
+        cxs2=vmem((half * h, h), BF16),
+        cxr2=vmem((half * h, h), BF16),
         cxs1=vmem((half, NP * cw, h), BF16),
         cxr1=vmem((half, NP * cw, h), BF16),
-        s1=vmem((half, NP, cw, h), BF16),
-        r1=vmem((half, NP, cw, h), BF16),
+        s1=vmem((NP, half * cw, h), BF16),
+        r1=vmem((NP, half * cw, h), BF16),
         zhs=vmem((half, cw, h), BF16),
         zhr=vmem((half, cw, h), BF16),
         d1s=vmem((half, cw, h), F32),
-        d1r=vmem((half, cw, h), F32),
-        bias=vmem((BIAS, h), F32),
+        bias=vmem((8, h), F32),
+        bs=vmem((1, h), F32),
+        br=vmem((1, h), F32),
+        bmine=vmem((1, h), F32),
+        btheirs=vmem((1, h), F32),
+        bplane=vmem((NP, 1, h), F32),
+        bcol=vmem((ZZ, 1, h), F32),
         loc=dma((5 + Z,)),
         own=dma((Z,)),
         xs=dma((Z,)),
         xr=dma((Z,)),
         hs=dma((Z,)),
         hr=dma((Z,)),
-        ss=dma((9 * half,)),
-        rs=dma((9 * half,)),
-        st=dma((2 * half + 3,)),
-    )
-    for q in range(half):
-        rows = hc + (BIAS if q == 0 else 0)
-        for name in ("s2", "r2", "ag", "agp"):
-            shapes[f"{name}_{q}"] = vmem((NP, rows, h), BF16)
-        shapes[f"zb_{q}"] = vmem((ZZ, rows, h), BF16)
+        ss=dma((PHASES * half * PARTS,)),
+        rs=dma((PHASES * half * PARTS,)),
+        st=dma((half * PARTS + 2,)),
+    )
+    for n in range(half * PARTS):
+        for name in ("s2", "r2", "ag"):
+            shapes[f"{name}_{n}"] = vmem((NP, hc // PARTS, h), BF16)
+        shapes[f"zb_{n}"] = vmem((ZZ, hc // PARTS, h), BF16)
     out1, out2, outb = pl.pallas_call(
         functools.partial(kernel, dims, factor, tuple(shapes)),
         name="graph_grads",
         out_shape=(
             jax.ShapeDtypeStruct((relations + 1, cw, h), F32),
             jax.ShapeDtypeStruct((relations + 1, NP, hc, h), BF16),
-            jax.ShapeDtypeStruct((BIAS, h), F32),
+            jax.ShapeDtypeStruct((8, h), F32),
         ),
         in_specs=[any_spec] * 6,
         out_specs=(any_spec,) * 3,
         scratch_shapes=list(shapes.values()),
         compiler_params=pltpu.CompilerParams(
-            collective_id=0, has_side_effects=True, vmem_limit_bytes=66000000
+            collective_id=0, has_side_effects=True, vmem_limit_bytes=MAIN_LIMIT
         ),
     )(features, adjacency_one, pre_hidden, adjacency_two, weight_two, out_grad)
-    return out1, outb[0], out2.reshape(relations + 1, h, h).astype(F32), outb[1]
+    panels = relations + 1
+    vmem_spec = pl.BlockSpec(memory_space=pltpu.VMEM)
+    first, second, bias_one, bias_two = pl.pallas_call(
+        widen,
+        name="widen",
+        out_shape=(
+            jax.ShapeDtypeStruct((panels, cw, h), F32),
+            jax.ShapeDtypeStruct((panels, NP, hc, h), F32),
+            jax.ShapeDtypeStruct((1, h), F32),
+            jax.ShapeDtypeStruct((1, h), F32),
+        ),
+        in_specs=[any_spec] * 3,
+        out_specs=(any_spec, any_spec, vmem_spec, vmem_spec),
+        scratch_shapes=[
+            vmem((panels, cw, h), F32),
+            vmem((panels, NP, hc, h), BF16),
+            vmem((panels, NP, hc, h), F32),
+            vmem((8, h), F32),
+            dma((panels + 2,)),
+            dma((panels + 1,)),
+        ],
+        compiler_params=pltpu.CompilerParams(vmem_limit_bytes=WIDEN_LIMIT),
+    )(out1, out2, outb)
+    return first, bias_one.reshape(h), second.reshape(panels, h, h), bias_two.reshape(h)
 
 
 def build(devices, dims):

time: 49.5 us -> 46.9 us (0.947)
  other arithmetic: 2.42 us -> 0 us
  local copies, waits for them, and re-layouts: 1.99 us -> 0 us
  Pallas kernels: 44.2 us -> 46.1 us
    pallas_call x0 -> x1, Pallas kernels: none -> 2.78 us  [on_device(): pl.pallas_call(widen, name='widen', out_shape=(jax.ShapeDtypeStruct((pane...]
    convert_element_type x1 -> x0, other arithmetic: 2.42 us -> none  [on_device(): out2.reshape(relations + 1, h, h).astype(F32)]
    slice x1 -> x0, local copies, waits for them, and re-layouts: 1.34 us -> none  [on_device(): outb[1]]
    pallas_call x1, Pallas kernels: 44.2 us -> 43.3 us  [on_device(): pl.pallas_call(functools.partial(kernel, dims, factor, tuple(shapes)), na...]
    unnamed x3 -> x0, local copies, waits for them, and re-layouts: 0.64 us -> none
where the time goes in v3:
time: 46.9 us; the launch traced here: 46.8 us
  Pallas kernels  46.1 us (98%)
  between operations  0.64 us (1%)
    pallas_call x1, Pallas kernels, on_device(): pl.pallas_call(functools.partial(kernel, dims, factor, tuple(shapes)), na...  43.3 us
    pallas_call x1, Pallas kernels, on_device(): pl.pallas_call(widen, name='widen', out_shape=(jax.ShapeDtypeStruct((pane...  2.78 us

profile of v3, /device:TPU:1, one launch (start us, length us, event | category | flops | bytes accessed | tf_op | source)
XLA Modules:
  0.0 46.8 jit_solution(6785179653011820226)
XLA Ops:
  0.6 43.3 %graph_grads.1 = (f32[6,16,256]{2,1,0:T(8,128)}, bf16[6,16,16,256]{3,2,1,0:T(8,128)(2,1)}, f32[8,256]{1,0:T(8,128)}) custom-call(bf16[1,64,16,512]{3,2,1,0:T(8,128)(2,1)} %feat.1, s32[1,64,5,16,512]{4,3,2,1,0:T(8,128)} %adj1.1, bf16[1,1,256,256]{3,2,1,0:T(8,128)(2,1)} %pre_any.1, s32[1,1,5,8,256]{4,3,2,1,0:T(8,128)} %adj2.1, bf16[6,256,256]{2,1,0:T(8,128)(2,1)} %w2_any.1, ...), custom_call_target="tpu_custom_call" | custom-call | tf_op jit(solution)/shard_map/graph_grads/pallas_call | solution.py:463
  44.0 2.8 %widen.1 = (f32[6,16,256]{2,1,0:T(8,128)}, f32[6,16,16,256]{3,2,1,0:T(8,128)}, f32[1,256]{1,0:T(1,128)}, f32[1,256]{1,0:T(1,128)}) custom-call(f32[6,16,256]{2,1,0:T(8,128)} %get-tuple-element.11.first_in, bf16[6,16,16,256]{3,2,1,0:T(8,128)(2,1)} %get-tuple-element.12.second_in, f32[8,256]{1,0:T(8,128)} %get-tuple-element.13.bias_in), custom_call_target="tpu_custom_call" | custom-call | tf_op jit(solution)/shard_map/widen/pallas_call | solution.py:480

commit v4 on v3

--- a/solution.py
+++ b/solution.py
@@ -18,10 +18,10 @@
 NN = (((1,), (0,)), ((), ()))
 NT = (((1,), (1,)), ((), ()))
 TN = (((0,), (0,)), ((), ()))
-WIDEN_LIMIT = 66000000
-MAIN_LIMIT = 66000000
+WIDEN_LIMIT = 16 * 2**20
+MAIN_LIMIT = 48 * 2**20
 TOP = 16
-PARTS = 1
+PAIR = 2
 PHASES = 13
 SWAP2, RS2, COL, AG, SWAP3, SWAP1, RS1, CROSS, SWAP4, BSWAP, BPLANE, BCOL, BLAST = range(PHASES)
 
@@ -73,22 +73,22 @@
     me = y * X + x
     zabs = g * Z + z
     relations = v.words1.shape[0] // Z
-    half = (relations + 1) // C
+    panels = relations + 1
+    count = panels // PAIR
+    half = panels // C
     cw = feat.shape[2]
     seeds, h = v.og.shape
     dst = v.pre.shape[0]
     hc = h // NP
-    chunks = [(q, p) for q in range(half) for p in range(PARTS)]
-    pc = hc // PARTS
     base = me * Z
     partner = (y, x, z, g, 1 - c)
     across = (y, x, z, 1 - g, c)
 
     def send_sem(phase, q=0):
-        return v.ss.at[phase * len(chunks) + q]
+        return v.ss.at[phase * count + q]
 
     def recv_sem(phase, q=0):
-        return v.rs.at[phase * len(chunks) + q]
+        return v.rs.at[phase * count + q]
 
     rows_of = [lax.rem(y + d, Y) for d in range(Y)]
     cols_of = [lax.rem(x + d, X) for d in range(X)]
@@ -184,17 +184,21 @@
     for r in range(relations):
         mixed = (mm(v.dense2[r], hidden, NN) * v.weight2[r]).astype(BF16)
         v.wg[r + 1] = mm(mixed, low, TN)
-    bias_one = jnp.sum(v.hgown[...].astype(F32), axis=0, keepdims=True)
-    bias_two = jnp.sum(scaled, axis=0, keepdims=True)
-    first = c == 0
-    bias_keep = jnp.where(first, bias_one, bias_two)
-    v.bs[...] = jnp.where(first, bias_two, bias_one)
-    for q in range(half):
-        v.cxs2[pl.ds(q * h, h), :] = v.wg[(1 - c) * half + q].astype(BF16)
-    swap2 = remote(v.cxs2, v.cxr2, send_sem(SWAP2), recv_sem(SWAP2), partner)
-    swap2.start()
-    bias_swap = remote(v.bs, v.br, send_sem(BSWAP), recv_sem(BSWAP), partner)
-    bias_swap.start()
+    v.bown[pl.ds(0, 1), :] = jnp.sum(v.hgown[...].astype(F32), axis=0, keepdims=True)
+    v.bown[pl.ds(1, 1), :] = jnp.sum(scaled, axis=0, keepdims=True)
+
+    def give_second():
+        return remote(v.cxs2, v.cxr2, send_sem(SWAP2), recv_sem(SWAP2), partner)
+
+    def give_bias():
+        return remote(v.bown, v.btheirs, send_sem(BSWAP), recv_sem(BSWAP), partner)
+
+    @pl.when(c == 0)
+    def _():
+        for q in range(panels):
+            v.cxs2[q] = v.wg[q].astype(BF16)
+        give_second().start()
+        give_bias().start()
 
     for load in loads[5:]:
         load.wait()
@@ -205,27 +209,30 @@
 
     lax.fori_loop(0, Z * relations, spread_one, 0)
 
-    bias_swap.wait_recv()
-    v.bplane[me] = bias_keep + v.br[...]
-    over_plane(
-        lambda slot, other, device: remote(
-            v.bplane.at[me], v.bplane.at[me], send_sem(BPLANE), recv_sem(BPLANE), device
-        ).start()
-    )
-    s2 = [getattr(v, f"s2_{n}") for n in range(len(chunks))]
-    r2 = [getattr(v, f"r2_{n}") for n in range(len(chunks))]
-    zb = [getattr(v, f"zb_{n}") for n in range(len(chunks))]
-    ag = [getattr(v, f"ag_{n}") for n in range(len(chunks))]
-    swap2.wait_recv()
-    for n, (q, p) in enumerate(chunks):
-        if p == 0:
-            both = (v.wg[c * half + q] + v.cxr2[pl.ds(q * h, h), :].astype(F32)).astype(BF16).reshape(NP, hc, h)
-        s2[n][...] = both[:, p * pc : (p + 1) * pc]
+    s2 = [getattr(v, f"s2_{n}") for n in range(count)]
+    r2 = [getattr(v, f"r2_{n}") for n in range(count)]
+    zb = [getattr(v, f"zb_{n}") for n in range(count)]
+    ag = [getattr(v, f"ag_{n}") for n in range(count)]
+
+    @pl.when(c == 1)
+    def _():
+        give_bias().wait_recv()
+        v.bplane[me] = v.bown[...] + v.btheirs[...]
         over_plane(
             lambda slot, other, device: remote(
-                s2[n].at[other], r2[n].at[slot], send_sem(RS2, n), recv_sem(RS2, n), device
+                v.bplane.at[me], v.bplane.at[me], send_sem(BPLANE), recv_sem(BPLANE), device
             ).start()
         )
+        give_second().wait_recv()
+        for n in range(count):
+            for p in range(PAIR):
+                both = v.wg[PAIR * n + p] + v.cxr2[PAIR * n + p].astype(F32)
+                s2[n][:, pl.ds(p * hc, hc), :] = both.astype(BF16).reshape(NP, hc, h)
+            over_plane(
+                lambda slot, other, device: remote(
+                    s2[n].at[other], r2[n].at[slot], send_sem(RS2, n), recv_sem(RS2, n), device
+                ).start()
+            )
 
     v.acc[...] = jnp.zeros_like(v.acc)
     least = lax.shift_left(1, lax.rem(lax.broadcasted_iota(jnp.int32, (1, dst), 1), 16)).astype(F32)
@@ -248,41 +255,32 @@
 
     lax.fori_loop(0, Z, one_minibatch, 0)
 
-    def swap1(q):
-        return remote(v.cxs1.at[q], v.cxr1.at[q], send_sem(SWAP1, q), recv_sem(SWAP1, q), partner)
+    def give_first():
+        return remote(v.cxs1, v.cxr1, send_sem(SWAP1), recv_sem(SWAP1), partner)
+
+    def result_two(n, p):
+        return remote(
+            ag[n].at[:, pl.ds(p * hc, hc), :],
+            out2.at[PAIR * n + p],
+            v.ps.at[PAIR * n + p],
+            v.pr.at[PAIR * n + p],
+            partner,
+        )
+
+    def store_two(n, p):
+        return local(ag[n].at[:, pl.ds(p * hc, hc), :], out2.at[PAIR * n + p], v.st.at[PAIR * n + p])
+
+    def result_bias():
+        return remote(v.bias, outb, send_sem(BLAST), recv_sem(BLAST), partner)
+
+    def landed(ref, sem):
+        local(ref, ref, sem).wait()
 
     for q in range(half):
         v.cxs1[q] = v.acc[(1 - c) * half + q].astype(BF16)
-        swap1(q).start()
-
-    def second_sum(q):
-        arrived = r2[q].at[pl.ds(1, NP - 1)]
-        local(arrived, arrived, recv_sem(RS2, q)).wait()
-        summed = s2[q][me].astype(F32)
-        for k in range(1, NP):
-            summed += r2[q][k].astype(F32)
-        zb[q][zabs] = summed.astype(BF16)
-        over_column(
-            lambda device: remote(
-                zb[q].at[zabs], zb[q].at[zabs], send_sem(COL, q), recv_sem(COL, q), device
-            ).start()
-        )
-
-    def column_sum(q):
-        arrived = zb[q].at[pl.ds(0, ZZ - 1)]
-        local(arrived, arrived, recv_sem(COL, q)).wait()
-        summed = zb[q][0].astype(F32)
-        for k in range(1, ZZ):
-            summed += zb[q][k].astype(F32)
-        ag[q][me] = summed.astype(BF16)
-        over_plane(
-            lambda slot, other, device: remote(
-                ag[q].at[me], ag[q].at[me], send_sem(AG, q), recv_sem(AG, q), device
-            ).start()
-        )
-
+    give_first().start()
+    give_first().wait_recv()
     for q in range(half):
-        swap1(q).wait_recv()
         both = v.acc[c * half + q] + v.cxr1[q].astype(F32)
         v.s1[:, pl.ds(q * cw, cw), :] = both.astype(BF16).reshape(NP, cw, h)
     over_plane(
@@ -292,110 +290,110 @@
         -1,
     )
 
-    for n in range(len(chunks)):
-        second_sum(n)
-    bias_in = v.bplane.at[pl.ds(0, NP - 1)]
-    local(bias_in, bias_in, recv_sem(BPLANE)).wait()
-    v.bcol[zabs] = jnp.sum(v.bplane[...], axis=0)
-    over_column(
-        lambda device: remote(
-            v.bcol.at[zabs], v.bcol.at[zabs], send_sem(BCOL), recv_sem(BCOL), device
-        ).start()
-    )
-
-    for n in range(len(chunks)):
-        column_sum(n)
-
-    first_in = v.r1.at[pl.ds(1, NP - 1)]
-    local(first_in, first_in, recv_sem(RS1)).wait()
+    @pl.when(c == 1)
+    def _():
+        for n in range(count):
+            landed(r2[n].at[pl.ds(1, NP - 1)], recv_sem(RS2, n))
+            summed = s2[n][me].astype(F32)
+            for k in range(1, NP):
+                summed += r2[n][k].astype(F32)
+            zb[n][zabs] = summed.astype(BF16)
+            over_column(
+                lambda device: remote(
+                    zb[n].at[zabs], zb[n].at[zabs], send_sem(COL, n), recv_sem(COL, n), device
+                ).start()
+            )
+        landed(v.bplane.at[pl.ds(0, NP - 1)], recv_sem(BPLANE))
+        v.bcol[zabs] = jnp.sum(v.bplane[...], axis=0)
+        over_column(
+            lambda device: remote(
+                v.bcol.at[zabs], v.bcol.at[zabs], send_sem(BCOL), recv_sem(BCOL), device
+            ).start()
+        )
+        for n in range(count):
+            landed(zb[n].at[pl.ds(0, ZZ - 1)], recv_sem(COL, n))
+            summed = zb[n][0].astype(F32)
+            for k in range(1, ZZ):
+                summed += zb[n][k].astype(F32)
+            ag[n][me] = summed.astype(BF16)
+            over_plane(
+                lambda slot, other, device: remote(
+                    ag[n].at[me], ag[n].at[me], send_sem(AG, n), recv_sem(AG, n), device
+                ).start()
+            )
+
+    landed(v.r1.at[pl.ds(1, NP - 1)], recv_sem(RS1))
     summed = v.s1[0].astype(F32)
     for k in range(1, NP):
         summed += v.r1[k].astype(F32)
     v.zhs[...] = summed.astype(BF16).reshape(half, cw, h)
     cross = remote(v.zhs, v.zhr, send_sem(CROSS), recv_sem(CROSS), across)
     cross.start()
-    bias_col = v.bcol.at[pl.ds(0, ZZ - 1)]
-    local(bias_col, bias_col, recv_sem(BCOL)).wait()
-    v.bmine[...] = jnp.sum(v.bcol[...], axis=0)
-    bias_last = remote(v.bmine, v.btheirs, send_sem(BLAST), recv_sem(BLAST), partner)
-    bias_last.start()
-
-    def panel_part(n):
-        q, p = chunks[n]
-        return out2.at[c * half + q, :, pl.ds(p * pc, pc), :]
-
-    def swap3(n):
-        return remote(ag[n], panel_part(n), send_sem(SWAP3, n), recv_sem(SWAP3, n), partner)
-
-    stores = []
-
-    def store(src, dst_ref):
-        stores.append(local(src, dst_ref, v.st.at[len(stores)]))
-        stores[-1].start()
-
-    for n in range(len(chunks)):
-        arrived = ag[n].at[pl.ds(0, NP - 1)]
-        local(arrived, arrived, recv_sem(AG, n)).wait()
-        swap3(n).start()
-        store(ag[n], panel_part(n))
+
+    @pl.when(c == 1)
+    def _():
+        landed(v.bcol.at[pl.ds(0, ZZ - 1)], recv_sem(BCOL))
+        v.bias[...] = jnp.sum(v.bcol[...], axis=0)
+        result_bias().start()
+        local(v.bias, outb, v.st.at[panels]).start()
+        for n in range(count):
+            landed(ag[n].at[pl.ds(0, NP - 1)], recv_sem(AG, n))
+            for p in range(PAIR):
+                result_two(n, p).start()
+                store_two(n, p).start()
 
     cross.wait_recv()
     v.d1s[...] = v.zhs[...].astype(F32) + v.zhr[...].astype(F32)
-    swap4 = remote(v.d1s, out1.at[pl.ds(c * half, half)], send_sem(SWAP4), recv_sem(SWAP4), partner)
-    swap4.start()
-    store(v.d1s, out1.at[pl.ds(c * half, half)])
-
-    bias_last.wait_recv()
-    mine, theirs = v.bmine[...], v.btheirs[...]
-    row = lax.broadcasted_iota(jnp.int32, (8, h), 0)
-    v.bias[...] = jnp.where(row == c, mine, theirs)
-    store(v.bias, outb)
-
-    for n in range(len(chunks)):
-        swap3(n).wait_recv()
-
-    swap4.wait_recv()
+    result_one = remote(v.d1s, out1.at[pl.ds(c * half, half)], send_sem(SWAP4), recv_sem(SWAP4), partner)
+    result_one.start()
+    store_one = local(v.d1s, out1.at[pl.ds(c * half, half)], v.so)
+    store_one.start()
+
+    give_first().wait_send()
+    landed(v.r1.at[pl.ds(1, NP - 1)], send_sem(RS1))
+    cross.wait_send()
+
+    @pl.when(c == 1)
+    def _():
+        landed(v.bplane.at[pl.ds(0, NP - 1)], send_sem(BPLANE))
+        landed(v.bcol.at[pl.ds(0, ZZ - 1)], send_sem(BCOL))
+        for n in range(count):
+            landed(r2[n].at[pl.ds(1, NP - 1)], send_sem(RS2, n))
+            landed(zb[n].at[pl.ds(0, ZZ - 1)], send_sem(COL, n))
+            landed(ag[n].at[pl.ds(0, NP - 1)], send_sem(AG, n))
+        result_bias().wait_send()
+        local(v.bias, outb, v.st.at[panels]).wait()
+        for q in range(panels):
+            store_two(q // PAIR, q % PAIR).wait()
+            result_two(q // PAIR, q % PAIR).wait_send()
+
+    @pl.when(c == 0)
+    def _():
+        give_second().wait_send()
+        give_bias().wait_send()
+        result_bias().wait_recv()
+        for q in range(panels):
+            result_two(q // PAIR, q % PAIR).wait_recv()
+
+    store_one.wait()
+    result_one.wait()
 
     for i in range(Z):
-        sent = v.xv.at[pl.ds(0, NP - 1)]
-        local(sent, sent, v.xs.at[i]).wait()
+        landed(v.xv.at[pl.ds(0, NP - 1)], v.xs.at[i])
     for k in range(1, Z):
         give_grad(k).wait_send()
-    for swap in (swap2, cross, swap4, bias_swap, bias_last):
-        swap.wait_send()
-    for q in range(half):
-        swap1(q).wait_send()
-    for n in range(len(chunks)):
-        swap3(n).wait_send()
-        for phase, ref in (
-            (RS2, r2[n].at[pl.ds(1, NP - 1)]),
-            (COL, zb[n].at[pl.ds(0, ZZ - 1)]),
-            (AG, ag[n].at[pl.ds(0, NP - 1)]),
-        ):
-            local(ref, ref, send_sem(phase, n)).wait()
-    local(bias_in, bias_in, send_sem(BPLANE)).wait()
-    local(bias_col, bias_col, send_sem(BCOL)).wait()
-    local(first_in, first_in, send_sem(RS1)).wait()
-    for copy in stores:
-        copy.wait()
-
-
-def widen(first_in, second_in, bias_in, first, second, bias_one, bias_two, one, low, wide, bias, come, go):
-    panels = low.shape[0]
-    gets = [local(second_in.at[r], low.at[r], come.at[r]) for r in range(panels)]
-    gets += [local(first_in, one, come.at[panels]), local(bias_in, bias, come.at[panels + 1])]
-    puts = [local(wide.at[r], second.at[r], go.at[r]) for r in range(panels)] + [local(one, first, go.at[panels])]
-    for get in gets:
-        get.start()
+
+
+def widen(first_in, second_in, bias_in, first, second, bias_one, bias_two, wide, go):
+    panels = second_in.shape[0]
+    puts = [local(wide.at[r], second.at[r], go.at[r]) for r in range(panels)]
+    puts.append(local(first_in, first, go.at[panels]))
+    puts[panels].start()
     for r in range(panels):
-        gets[r].wait()
-        wide[r] = low[r].astype(F32)
+        wide[r] = second_in[r].astype(F32)
         puts[r].start()
-    gets[panels].wait()
-    puts[panels].start()
-    gets[panels + 1].wait()
-    bias_one[...] = bias[:1]
-    bias_two[...] = bias[1:2]
+    bias_one[...] = bias_in[:1]
+    bias_two[...] = bias_in[1:2]
     for put in puts:
         put.wait()
 
@@ -407,8 +405,10 @@
     relations, word_rows = adjacency_one.shape[2:4]
     dst, h = pre_hidden.shape[2:]
     seeds = out_grad.shape[2]
-    half = (relations + 1) // C
     hc = h // NP
+    panels = relations + 1
+    count = panels // PAIR
+    half = panels // C
     factor = float(seeds * NP * ZZ * C) ** (-0.5)
     vmem = pltpu.VMEM
     any_spec = pl.BlockSpec(memory_space=pl.ANY)
@@ -430,8 +430,8 @@
         weight2=vmem((relations, seeds, dst), F32),
         acc=vmem((relations + 1, NP * cw, h), F32),
         wg=vmem((relations + 1, h, h), F32),
-        cxs2=vmem((half * h, h), BF16),
-        cxr2=vmem((half * h, h), BF16),
+        cxs2=vmem((panels, h, h), BF16),
+        cxr2=vmem((panels, h, h), BF16),
         cxs1=vmem((half, NP * cw, h), BF16),
         cxr1=vmem((half, NP * cw, h), BF16),
         s1=vmem((NP, half * cw, h), BF16),
@@ -439,34 +439,35 @@
         zhs=vmem((half, cw, h), BF16),
         zhr=vmem((half, cw, h), BF16),
         d1s=vmem((half, cw, h), F32),
-        bias=vmem((8, h), F32),
-        bs=vmem((1, h), F32),
-        br=vmem((1, h), F32),
-        bmine=vmem((1, h), F32),
-        btheirs=vmem((1, h), F32),
-        bplane=vmem((NP, 1, h), F32),
-        bcol=vmem((ZZ, 1, h), F32),
+        bias=vmem((2, h), F32),
+        bown=vmem((2, h), F32),
+        btheirs=vmem((2, h), F32),
+        bplane=vmem((NP, 2, h), F32),
+        bcol=vmem((ZZ, 2, h), F32),
         loc=dma((5 + Z,)),
         own=dma((Z,)),
         xs=dma((Z,)),
         xr=dma((Z,)),
         hs=dma((Z,)),
         hr=dma((Z,)),
-        ss=dma((PHASES * half * PARTS,)),
-        rs=dma((PHASES * half * PARTS,)),
-        st=dma((half * PARTS + 2,)),
+        ss=dma((PHASES * count,)),
+        rs=dma((PHASES * count,)),
+        ps=dma((panels,)),
+        pr=dma((panels,)),
+        st=dma((panels + 1,)),
+        so=pltpu.SemaphoreType.DMA,
     )
-    for n in range(half * PARTS):
+    for n in range(count):
         for name in ("s2", "r2", "ag"):
-            shapes[f"{name}_{n}"] = vmem((NP, hc // PARTS, h), BF16)
-        shapes[f"zb_{n}"] = vmem((ZZ, hc // PARTS, h), BF16)
+            shapes[f"{name}_{n}"] = vmem((NP, PAIR * hc, h), BF16)
+        shapes[f"zb_{n}"] = vmem((ZZ, PAIR * hc, h), BF16)
     out1, out2, outb = pl.pallas_call(
         functools.partial(kernel, dims, factor, tuple(shapes)),
         name="graph_grads",
         out_shape=(
             jax.ShapeDtypeStruct((relations + 1, cw, h), F32),
             jax.ShapeDtypeStruct((relations + 1, NP, hc, h), BF16),
-            jax.ShapeDtypeStruct((8, h), F32),
+            jax.ShapeDtypeStruct((2, h), F32),
         ),
         in_specs=[any_spec] * 6,
         out_specs=(any_spec,) * 3,
@@ -474,8 +475,12 @@
         compiler_params=pltpu.CompilerParams(
             collective_id=0, has_side_effects=True, vmem_limit_bytes=MAIN_LIMIT
         ),
-    )(features, adjacency_one, pre_hidden, adjacency_two, weight_two, out_grad)
-    panels = relations + 1
+    )(
+        *(
+            pltpu.with_memory_space_constraint(a, pltpu.HBM)
+            for a in (features, adjacency_one, pre_hidden, adjacency_two, weight_two, out_grad)
+        )
+    )
     vmem_spec = pl.BlockSpec(memory_space=pltpu.VMEM)
     first, second, bias_one, bias_two = pl.pallas_call(
         widen,
@@ -486,14 +491,10 @@
             jax.ShapeDtypeStruct((1, h), F32),
             jax.ShapeDtypeStruct((1, h), F32),
         ),
-        in_specs=[any_spec] * 3,
+        in_specs=[vmem_spec] * 3,
         out_specs=(any_spec, any_spec, vmem_spec, vmem_spec),
         scratch_shapes=[
-            vmem((panels, cw, h), F32),
-            vmem((panels, NP, hc, h), BF16),
             vmem((panels, NP, hc, h), F32),
-            vmem((8, h), F32),
-            dma((panels + 2,)),
             dma((panels + 1,)),
         ],
         compiler_params=pltpu.CompilerParams(vmem_limit_bytes=WIDEN_LIMIT),

time: 46.9 us -> 45 us (0.959)
  Pallas kernels: 46.1 us -> 44.2 us
    pallas_call x1, Pallas kernels: 2.78 us -> 1.8 us  [on_device(): pl.pallas_call(widen, name='widen', out_shape=(jax.ShapeDtypeStruct((pane...]
    pallas_call x1, Pallas kernels: 43.3 us -> 42.4 us  [on_device(): pl.pallas_call(functools.partial(kernel, dims, factor, tuple(shapes)), na...]
where the time goes in v4:
time: 45 us; the launch traced here: 44.9 us
  Pallas kernels  44.2 us (98%)
  between operations  0.64 us (1%)
    pallas_call x1, Pallas kernels, on_device(): pl.pallas_call(functools.partial(kernel, dims, factor, tuple(shapes)), na...  42.4 us
    pallas_call x1, Pallas kernels, on_device(): pl.pallas_call(widen, name='widen', out_shape=(jax.ShapeDtypeStruct((pane...  1.8 us

profile of v4, /device:TPU:1, one launch (start us, length us, event | category | flops | bytes accessed | tf_op | source)
XLA Modules:
  0.0 44.9 jit_solution(226397866989482619)
XLA Ops:
  0.6 42.4 %graph_grads.1 = (f32[6,16,256]{2,1,0:T(8,128)S(1)}, bf16[6,16,16,256]{3,2,1,0:T(8,128)(2,1)S(1)}, f32[2,256]{1,0:T(2,128)S(1)}) custom-call(bf16[1,64,16,512]{3,2,1,0:T(8,128)(2,1)} %feat.1, s32[1,64,5,16,512]{4,3,2,1,0:T(8,128)} %adj1.1, bf16[1,1,256,256]{3,2,1,0:T(8,128)(2,1)} %pre_any.1, s32[1,1,5,8,256]{4,3,2,1,0:T(8,128)} %adj2.1, ...), custom_call_target="tpu_custom_call" | custom-call | tf_op jit(solution)/shard_map/graph_grads/pallas_call | solution.py:464
  43.1 1.8 %widen.1 = (f32[6,16,256]{2,1,0:T(8,128)}, f32[6,16,16,256]{3,2,1,0:T(8,128)}, f32[1,256]{1,0:T(1,128)}, f32[1,256]{1,0:T(1,128)}) custom-call(f32[6,16,256]{2,1,0:T(8,128)S(1)} %get-tuple-element.11.first_in, bf16[6,16,16,256]{3,2,1,0:T(8,128)(2,1)S(1)} %get-tuple-element.12.second_in, f32[2,256]{1,0:T(2,128)S(1)} %get-tuple-element.13.bias_in), custom_call_target="tpu_custom_call" | custom-call | tf_op jit(solution)/shard_map/widen/pallas_call | solution.py:485

commit v5 on v4

--- a/solution.py
+++ b/solution.py
@@ -279,16 +279,6 @@
     for q in range(half):
         v.cxs1[q] = v.acc[(1 - c) * half + q].astype(BF16)
     give_first().start()
-    give_first().wait_recv()
-    for q in range(half):
-        both = v.acc[c * half + q] + v.cxr1[q].astype(F32)
-        v.s1[:, pl.ds(q * cw, cw), :] = both.astype(BF16).reshape(NP, cw, h)
-    over_plane(
-        lambda slot, other, device: remote(
-            v.s1.at[slot], v.r1.at[slot], send_sem(RS1), recv_sem(RS1), device
-        ).start(),
-        -1,
-    )
 
     @pl.when(c == 1)
     def _():
@@ -310,6 +300,20 @@
                 v.bcol.at[zabs], v.bcol.at[zabs], send_sem(BCOL), recv_sem(BCOL), device
             ).start()
         )
+
+    give_first().wait_recv()
+    for q in range(half):
+        both = v.acc[c * half + q] + v.cxr1[q].astype(F32)
+        v.s1[:, pl.ds(q * cw, cw), :] = both.astype(BF16).reshape(NP, cw, h)
+    over_plane(
+        lambda slot, other, device: remote(
+            v.s1.at[slot], v.r1.at[slot], send_sem(RS1), recv_sem(RS1), device
+        ).start(),
+        -1,
+    )
+
+    @pl.when(c == 1)
+    def _():
         for n in range(count):
             landed(zb[n].at[pl.ds(0, ZZ - 1)], recv_sem(COL, n))
             summed = zb[n][0].astype(F32)

time: 45 us -> 43.8 us (0.973)
  Pallas kernels: 44.2 us -> 43 us
    pallas_call x1, Pallas kernels: 42.4 us -> 41.3 us  [on_device(): pl.pallas_call(functools.partial(kernel, dims, factor, tuple(shapes)), na...]
where the time goes in v5:
time: 43.8 us; the launch traced here: 43.7 us
  Pallas kernels  43 us (98%)
  between operations  0.64 us (1%)
    pallas_call x1, Pallas kernels, on_device(): pl.pallas_call(functools.partial(kernel, dims, factor, tuple(shapes)), na...  41.3 us
    pallas_call x1, Pallas kernels, on_device(): pl.pallas_call(widen, name='widen', out_shape=(jax.ShapeDtypeStruct((pane...  1.8 us

profile of v5, /device:TPU:1, one launch (start us, length us, event | category | flops | bytes accessed | tf_op | source)
XLA Modules:
  0.0 43.7 jit_solution(6781142505210244224)
XLA Ops:
  0.6 41.3 %graph_grads.1 = (f32[6,16,256]{2,1,0:T(8,128)S(1)}, bf16[6,16,16,256]{3,2,1,0:T(8,128)(2,1)S(1)}, f32[2,256]{1,0:T(2,128)S(1)}) custom-call(bf16[1,64,16,512]{3,2,1,0:T(8,128)(2,1)} %feat.1, s32[1,64,5,16,512]{4,3,2,1,0:T(8,128)} %adj1.1, bf16[1,1,256,256]{3,2,1,0:T(8,128)(2,1)} %pre_any.1, s32[1,1,5,8,256]{4,3,2,1,0:T(8,128)} %adj2.1, ...), custom_call_target="tpu_custom_call" | custom-call | tf_op jit(solution)/shard_map/graph_grads/pallas_call | solution.py:468
  41.9 1.8 %widen.1 = (f32[6,16,256]{2,1,0:T(8,128)}, f32[6,16,16,256]{3,2,1,0:T(8,128)}, f32[1,256]{1,0:T(1,128)}, f32[1,256]{1,0:T(1,128)}) custom-call(f32[6,16,256]{2,1,0:T(8,128)S(1)} %get-tuple-element.11.first_in, bf16[6,16,16,256]{3,2,1,0:T(8,128)(2,1)S(1)} %get-tuple-element.12.second_in, f32[2,256]{1,0:T(2,128)S(1)} %get-tuple-element.13.bias_in), custom_call_target="tpu_custom_call" | custom-call | tf_op jit(solution)/shard_map/widen/pallas_call | solution.py:489

commit v6 on v5

--- a/solution.py
+++ b/solution.py
@@ -22,8 +22,10 @@
 MAIN_LIMIT = 48 * 2**20
 TOP = 16
 PAIR = 2
-PHASES = 13
-SWAP2, RS2, COL, AG, SWAP3, SWAP1, RS1, CROSS, SWAP4, BSWAP, BPLANE, BCOL, BLAST = range(PHASES)
+CHUNKED = 3
+SINGLE = 9
+RS2, COL, AG = range(CHUNKED)
+SWAP2, SWAP1, RS1, CROSS, SWAP4, BSWAP, BPLANE, BCOL, BLAST = range(CHUNKED, CHUNKED + SINGLE)
 
 
 def mm(a, b, dims):
@@ -84,11 +86,14 @@
     partner = (y, x, z, g, 1 - c)
     across = (y, x, z, 1 - g, c)
 
-    def send_sem(phase, q=0):
-        return v.ss.at[phase * count + q]
-
-    def recv_sem(phase, q=0):
-        return v.rs.at[phase * count + q]
+    def place(phase, n):
+        return phase * count + n if phase < CHUNKED else CHUNKED * (count - 1) + phase
+
+    def send_sem(phase, n=0):
+        return v.ss.at[phase]
+
+    def recv_sem(phase, n=0):
+        return v.rs.at[place(phase, n)]
 
     rows_of = [lax.rem(y + d, Y) for d in range(Y)]
     cols_of = [lax.rem(x + d, X) for d in range(X)]
@@ -128,7 +133,7 @@
     ]
     for q in range(Z):
         loads.append(
-            local(adj1.at[0, base + q], v.words1.at[pl.ds(q * relations, relations)], v.loc.at[5 + q])
+            local(adj1.at[0, base + q], v.words1.at[pl.ds(q * relations, relations)], v.loc.at[5])
         )
     for load in loads:
         load.start()
@@ -156,19 +161,19 @@
     pl.semaphore_wait(barrier, NP + ZZ - 1)
 
     def give_grad(k):
-        return remote(v.hgown, v.hgbuf.at[z], v.hs.at[k], v.hr.at[k], (y, x, minibatch(k), g, c))
+        return remote(v.hgown, v.hgbuf.at[z], v.hs.at[0], v.hr.at[k], (y, x, minibatch(k), g, c))
 
     for k in range(1, Z):
         give_grad(k).start()
 
     def send_features(i, carry):
         m = minibatch(i)
-        local(v.xv.at[base + m], v.rx.at[m, pl.ds(TOP, cw), :], v.own.at[i]).start()
+        local(v.xv.at[base + m], v.rx.at[m, pl.ds(TOP, cw), :], v.xr.at[i]).start()
         over_plane(
             lambda slot, other, device: remote(
                 v.xv.at[other * Z + m],
                 v.rx.at[m, pl.ds(TOP + slot * cw, cw), :],
-                v.xs.at[i],
+                v.xs.at[0],
                 v.xr.at[i],
                 device,
             ).start()
@@ -200,8 +205,7 @@
         give_second().start()
         give_bias().start()
 
-    for load in loads[5:]:
-        load.wait()
+    local(v.words1, v.words1, v.loc.at[5]).wait()
 
     def spread_one(t, carry):
         spread_scaled(v.words1, t, v.dense1, 16 * v.words1.shape[1], v.words1.shape[2])
@@ -209,10 +213,7 @@
 
     lax.fori_loop(0, Z * relations, spread_one, 0)
 
-    s2 = [getattr(v, f"s2_{n}") for n in range(count)]
-    r2 = [getattr(v, f"r2_{n}") for n in range(count)]
-    zb = [getattr(v, f"zb_{n}") for n in range(count)]
-    ag = [getattr(v, f"ag_{n}") for n in range(count)]
+    s2, r2, zb, ag = ([ref.at[n] for n in range(count)] for ref in (v.s2, v.r2, v.zb, v.ag))
 
     @pl.when(c == 1)
     def _():
@@ -239,8 +240,7 @@
 
     def one_minibatch(i, carry):
         m = minibatch(i)
-        local(v.xv.at[base + m], v.rx.at[m, pl.ds(TOP, cw), :], v.own.at[i]).wait()
-        arrived = v.rx.at[m, pl.ds(TOP + cw, (NP - 1) * cw), :]
+        arrived = v.rx.at[m, pl.ds(TOP, NP * cw), :]
         local(arrived, arrived, v.xr.at[i]).wait()
         local(v.hgown, v.hgbuf.at[m], v.hr.at[i]).wait()
         grad_m = v.hgbuf[m]
@@ -262,13 +262,13 @@
         return remote(
             ag[n].at[:, pl.ds(p * hc, hc), :],
             out2.at[PAIR * n + p],
-            v.ps.at[PAIR * n + p],
-            v.pr.at[PAIR * n + p],
+            v.ps.at[0],
+            v.ps.at[1],
             partner,
         )
 
     def store_two(n, p):
-        return local(ag[n].at[:, pl.ds(p * hc, hc), :], out2.at[PAIR * n + p], v.st.at[PAIR * n + p])
+        return local(ag[n].at[:, pl.ds(p * hc, hc), :], out2.at[PAIR * n + p], v.st.at[0])
 
     def result_bias():
         return remote(v.bias, outb, send_sem(BLAST), recv_sem(BLAST), partner)
@@ -339,7 +339,7 @@
         landed(v.bcol.at[pl.ds(0, ZZ - 1)], recv_sem(BCOL))
         v.bias[...] = jnp.sum(v.bcol[...], axis=0)
         result_bias().start()
-        local(v.bias, outb, v.st.at[panels]).start()
+        local(v.bias, outb, v.st.at[1]).start()
         for n in range(count):
             landed(ag[n].at[pl.ds(0, NP - 1)], recv_sem(AG, n))
             for p in range(PAIR):
@@ -361,43 +361,39 @@
     def _():
         landed(v.bplane.at[pl.ds(0, NP - 1)], send_sem(BPLANE))
         landed(v.bcol.at[pl.ds(0, ZZ - 1)], send_sem(BCOL))
-        for n in range(count):
-            landed(r2[n].at[pl.ds(1, NP - 1)], send_sem(RS2, n))
-            landed(zb[n].at[pl.ds(0, ZZ - 1)], send_sem(COL, n))
-            landed(ag[n].at[pl.ds(0, NP - 1)], send_sem(AG, n))
+        landed(v.r2.at[:, pl.ds(1, NP - 1)], send_sem(RS2))
+        landed(v.zb.at[:, pl.ds(0, ZZ - 1)], send_sem(COL))
+        landed(v.ag.at[:, pl.ds(0, NP - 1)], send_sem(AG))
         result_bias().wait_send()
-        local(v.bias, outb, v.st.at[panels]).wait()
-        for q in range(panels):
-            store_two(q // PAIR, q % PAIR).wait()
-            result_two(q // PAIR, q % PAIR).wait_send()
+        local(v.bias, outb, v.st.at[1]).wait()
+        landed(out2, v.st.at[0])
+        landed(out2, v.ps.at[0])
 
     @pl.when(c == 0)
     def _():
         give_second().wait_send()
         give_bias().wait_send()
         result_bias().wait_recv()
-        for q in range(panels):
-            result_two(q // PAIR, q % PAIR).wait_recv()
+        landed(out2, v.ps.at[1])
 
     store_one.wait()
     result_one.wait()
 
-    for i in range(Z):
-        landed(v.xv.at[pl.ds(0, NP - 1)], v.xs.at[i])
-    for k in range(1, Z):
-        give_grad(k).wait_send()
+    landed(v.xv.at[pl.ds(0, Z * (NP - 1))], v.xs.at[0])
+    landed(v.hgbuf.at[pl.ds(0, Z - 1)], v.hs.at[0])
 
 
 def widen(first_in, second_in, bias_in, first, second, bias_one, bias_two, wide, go):
     panels = second_in.shape[0]
     puts = [local(wide.at[r], second.at[r], go.at[r]) for r in range(panels)]
     puts.append(local(first_in, first, go.at[panels]))
-    puts[panels].start()
+    puts.append(local(bias_in.at[pl.ds(0, 1)], bias_one, go.at[panels + 1]))
+    puts.append(local(bias_in.at[pl.ds(1, 1)], bias_two, go.at[panels + 2]))
+    for put in puts[panels:]:
+        put.start()
     for r in range(panels):
         wide[r] = second_in[r].astype(F32)
         puts[r].start()
-    bias_one[...] = bias_in[:1]
-    bias_two[...] = bias_in[1:2]
     for put in puts:
         put.wait()
 
@@ -448,23 +444,20 @@
         btheirs=vmem((2, h), F32),
         bplane=vmem((NP, 2, h), F32),
         bcol=vmem((ZZ, 2, h), F32),
-        loc=dma((5 + Z,)),
-        own=dma((Z,)),
-        xs=dma((Z,)),
+        loc=dma((6,)),
+        xs=dma((1,)),
         xr=dma((Z,)),
-        hs=dma((Z,)),
+        hs=dma((1,)),
         hr=dma((Z,)),
-        ss=dma((PHASES * count,)),
-        rs=dma((PHASES * count,)),
-        ps=dma((panels,)),
-        pr=dma((panels,)),
-        st=dma((panels + 1,)),
+        ss=dma((CHUNKED + SINGLE,)),
+        rs=dma((CHUNKED * count + SINGLE,)),
+        ps=dma((2,)),
+        st=dma((2,)),
         so=pltpu.SemaphoreType.DMA,
     )
-    for n in range(count):
-        for name in ("s2", "r2", "ag"):
-            shapes[f"{name}_{n}"] = vmem((NP, PAIR * hc, h), BF16)
-        shapes[f"zb_{n}"] = vmem((ZZ, PAIR * hc, h), BF16)
+    for name in ("s2", "r2", "ag"):
+        shapes[name] = vmem((count, NP, PAIR * hc, h), BF16)
+    shapes["zb"] = vmem((count, ZZ, PAIR * hc, h), BF16)
     out1, out2, outb = pl.pallas_call(
         functools.partial(kernel, dims, factor, tuple(shapes)),
         name="graph_grads",
@@ -496,10 +489,10 @@
             jax.ShapeDtypeStruct((1, h), F32),
         ),
         in_specs=[vmem_spec] * 3,
-        out_specs=(any_spec, any_spec, vmem_spec, vmem_spec),
+        out_specs=(any_spec,) * 4,
         scratch_shapes=[
             vmem((panels, NP, hc, h), F32),
-            dma((panels + 1,)),
+            dma((panels + 3,)),
         ],
         compiler_params=pltpu.CompilerParams(vmem_limit_bytes=WIDEN_LIMIT),
     )(out1, out2, outb)

time: 43.8 us -> 42.6 us (0.973)
  Pallas kernels: 43 us -> 41.8 us
    pallas_call x1, Pallas kernels: 41.3 us -> 40.6 us  [on_device(): pl.pallas_call(functools.partial(kernel, dims, factor, tuple(shapes)), na...]
    pallas_call x1, Pallas kernels: 1.8 us -> 1.26 us  [on_device(): pl.pallas_call(widen, name='widen', out_shape=(jax.ShapeDtypeStruct((pane...]
where the time goes in v6:
time: 42.6 us; the launch traced here: 42.5 us
  Pallas kernels  41.8 us (98%)
  between operations  0.64 us (2%)
    pallas_call x1, Pallas kernels, on_device(): pl.pallas_call(functools.partial(kernel, dims, factor, tuple(shapes)), na...  40.6 us
    pallas_call x1, Pallas kernels, on_device(): pl.pallas_call(widen, name='widen', out_shape=(jax.ShapeDtypeStruct((pane...  1.26 us

profile of v6, /device:TPU:1, one launch (start us, length us, event | category | flops | bytes accessed | tf_op | source)
XLA Modules:
  0.0 42.5 jit_solution(6729329585799936979)
XLA Ops:
  0.6 40.6 %graph_grads.1 = (f32[6,16,256]{2,1,0:T(8,128)S(1)}, bf16[6,16,16,256]{3,2,1,0:T(8,128)(2,1)S(1)}, f32[2,256]{1,0:T(2,128)S(1)}) custom-call(bf16[1,64,16,512]{3,2,1,0:T(8,128)(2,1)} %feat.1, s32[1,64,5,16,512]{4,3,2,1,0:T(8,128)} %adj1.1, bf16[1,1,256,256]{3,2,1,0:T(8,128)(2,1)} %pre_any.1, s32[1,1,5,8,256]{4,3,2,1,0:T(8,128)} %adj2.1, ...), custom_call_target="tpu_custom_call" | custom-call | tf_op jit(solution)/shard_map/graph_grads/pallas_call | solution.py:461
  41.2 1.3 %widen.1 = (f32[6,16,256]{2,1,0:T(8,128)}, f32[6,16,16,256]{3,2,1,0:T(8,128)}, f32[1,256]{1,0:T(1,128)}, f32[1,256]{1,0:T(1,128)}) custom-call(f32[6,16,256]{2,1,0:T(8,128)S(1)} %get-tuple-element.11.first_in, bf16[6,16,16,256]{3,2,1,0:T(8,128)(2,1)S(1)} %get-tuple-element.12.second_in, f32[2,256]{1,0:T(2,128)S(1)} %get-tuple-element.13.bias_in), custom_call_target="tpu_custom_call" | custom-call | tf_op jit(solution)/shard_map/widen/pallas_call | solution.py:482

commit v7 on v6

--- a/solution.py
+++ b/solution.py
@@ -142,6 +142,25 @@
     for r in range(relations):
         spread_bits(v.words2, r, v.dense2, seeds, h)
 
+    loads[4].wait()
+    pl.semaphore_wait(barrier, NP + ZZ - 1)
+
+    def send_features(i, carry):
+        m = minibatch(i)
+        local(v.xv.at[base + m], v.rx.at[m, pl.ds(TOP, cw), :], v.xr.at[i]).start()
+        over_plane(
+            lambda slot, other, device: remote(
+                v.xv.at[other * Z + m],
+                v.rx.at[m, pl.ds(TOP + slot * cw, cw), :],
+                v.xs.at[0],
+                v.xr.at[i],
+                device,
+            ).start()
+        )
+        return carry
+
+    lax.fori_loop(0, Z, send_features, 0)
+
     for load in loads[1:4]:
         load.wait()
     scaled = v.og[...].astype(F32) * factor
@@ -156,31 +175,12 @@
         v.total[...] += mm(v.dense2[r], backed, TN)
     v.hgown[...] = jnp.where(v.pre[...] > 0, v.total[...], 0.0).astype(BF16)
     local(v.hgown, v.hgbuf.at[z], v.hr.at[0]).start()
-    loads[4].wait()
-
-    pl.semaphore_wait(barrier, NP + ZZ - 1)
 
     def give_grad(k):
         return remote(v.hgown, v.hgbuf.at[z], v.hs.at[0], v.hr.at[k], (y, x, minibatch(k), g, c))
 
     for k in range(1, Z):
         give_grad(k).start()
-
-    def send_features(i, carry):
-        m = minibatch(i)
-        local(v.xv.at[base + m], v.rx.at[m, pl.ds(TOP, cw), :], v.xr.at[i]).start()
-        over_plane(
-            lambda slot, other, device: remote(
-                v.xv.at[other * Z + m],
-                v.rx.at[m, pl.ds(TOP + slot * cw, cw), :],
-                v.xs.at[0],
-                v.xr.at[i],
-                device,
-            ).start()
-        )
-        return carry
-
-    lax.fori_loop(0, Z, send_features, 0)
 
     hidden = jnp.maximum(v.pre[...], 0)
     scaled = v.og[...].astype(F32) * factor

time: 42.6 us -> 42.3 us (level)
  no operation moved by 1% of the time
where the time goes in v7:
time: 42.3 us; the launch traced here: 42.1 us
  Pallas kernels  41.5 us (98%)
  between operations  0.64 us (2%)
    pallas_call x1, Pallas kernels, on_device(): pl.pallas_call(functools.partial(kernel, dims, factor, tuple(shapes)), na...  40.2 us
    pallas_call x1, Pallas kernels, on_device(): pl.pallas_call(widen, name='widen', out_shape=(jax.ShapeDtypeStruct((pane...  1.26 us

profile of v7, /device:TPU:1, one launch (start us, length us, event | category | flops | bytes accessed | tf_op | source)
XLA Modules:
  0.0 42.1 jit_solution(7808948573006713334)
XLA Ops:
  0.6 40.2 %graph_grads.1 = (f32[6,16,256]{2,1,0:T(8,128)S(1)}, bf16[6,16,16,256]{3,2,1,0:T(8,128)(2,1)S(1)}, f32[2,256]{1,0:T(2,128)S(1)}) custom-call(bf16[1,64,16,512]{3,2,1,0:T(8,128)(2,1)} %feat.1, s32[1,64,5,16,512]{4,3,2,1,0:T(8,128)} %adj1.1, bf16[1,1,256,256]{3,2,1,0:T(8,128)(2,1)} %pre_any.1, s32[1,1,5,8,256]{4,3,2,1,0:T(8,128)} %adj2.1, ...), custom_call_target="tpu_custom_call" | custom-call | tf_op jit(solution)/shard_map/graph_grads/pallas_call | solution.py:461
  40.9 1.3 %widen.1 = (f32[6,16,256]{2,1,0:T(8,128)}, f32[6,16,16,256]{3,2,1,0:T(8,128)}, f32[1,256]{1,0:T(1,128)}, f32[1,256]{1,0:T(1,128)}) custom-call(f32[6,16,256]{2,1,0:T(8,128)S(1)} %get-tuple-element.11.first_in, bf16[6,16,16,256]{3,2,1,0:T(8,128)(2,1)S(1)} %get-tuple-element.12.second_in, f32[2,256]{1,0:T(2,128)S(1)} %get-tuple-element.13.bias_in), custom_call_target="tpu_custom_call" | custom-call | tf_op jit(solution)/shard_map/widen/pallas_call | solution.py:482
